TPU v7x, 32 devices: a whole 2x2x4 slice. The times are simulated.
32 devices in a mesh: agg: 2 (over y), gx: 4 (over x, core), gy: 4 (over z).
Axes of the slice: x: 2, y: 2, z: 4, core: 2. Of those that a mesh axis runs over, the one named last changes fastest.
Arguments:
- velocity_prev: float32 [3, 32, 64, 256], P(None, 'gx', 'gy', 'agg'), may hold values from -6 to 6
- forcing: float32 [3, 32, 64, 256], P(None, 'gx', 'gy', 'agg'), may hold values from -6 to 6
- reaction: float32 [32, 64, 256], P('gx', 'gy', 'agg'), may hold values from 0.1 to 4
Outputs:
- velocity: float32 [3, 32, 64, 256], P(None, 'gx', 'gy', 'agg')
- compressed: float32 [3, 64, 256, 16], P(None, 'gy', ('agg', 'gx'))
All inputs are finite; a program needn't handle non-finite values.
Results may differ from a plain program's by a relative error of at most 0.00002.
Values sent between devices are 32-bit elements; how exact they have to be, the bound alone decides.
A program may use at most 64 MiB of HBM per device.

v0:
```python
import jax
import jax.numpy as jnp
from jax import lax
from jax.sharding import PartitionSpec as P

SWEEPS = 2
COARSE_SWEEPS = 4
LX = 5


damping = 0.8
root_half = 0.7071067811865476


def padded_2(block, sides, width):
    for axis, dim in sides:
        count = lax.axis_size(axis)
        forward = [(i, i + 1) for i in range(count - 1)]
        backward = [(target, source) for source, target in forward]
        low = lax.ppermute(
            lax.slice_in_dim(block, block.shape[dim] - width, None, axis=dim), axis, forward
        )
        high = lax.ppermute(lax.slice_in_dim(block, 0, width, axis=dim), axis, backward)
        block = jnp.concatenate([low, block, high], axis=dim)
    return block


def neighbours(padded):
    summed = padded[:, 2:, 1:-1, 1:-1] + padded[:, :-2, 1:-1, 1:-1]
    summed = summed + padded[:, 1:-1, 2:, 1:-1] + padded[:, 1:-1, :-2, 1:-1]
    summed = summed + padded[:, 1:-1, 1:-1, 2:] + padded[:, 1:-1, 1:-1, :-2]
    return summed


def trim_cells(values, depth):
    return values[:, depth:-depth, depth:-depth, depth:-depth]


def along_axis(count, depth, position, devices):
    spots = position * count + jnp.arange(count + 2 * depth, dtype=jnp.int32) - depth
    inside = (spots >= 0) & (spots < count * devices)
    return inside.astype(jnp.float32)


def valid_mask(cells_x, cells_y, cells_z, depth):
    mask_x = along_axis(cells_x, depth, lax.axis_index("gx"), lax.axis_size("gx"))
    mask_y = along_axis(cells_y, depth, lax.axis_index("gy"), lax.axis_size("gy"))
    mask_z = along_axis(cells_z, depth, lax.axis_index("agg"), lax.axis_size("agg"))
    return (mask_x[:, None, None] * mask_y[None, :, None] * mask_z[None, None, :])[None]


def last_residual(current, forcing, diagonal):
    padded = padded_2(current, (("agg", 3), ("gx", 1), ("gy", 2)), 1)
    return forcing - (diagonal * current - neighbours(padded))


def block_mean(field):
    components, size_x, size_y, size_z = field.shape
    return field.reshape(components, size_x // 2, 2, size_y // 2, 2, size_z // 2, 2).mean(
        axis=(2, 4, 6)
    )


def prolong(coarse):
    components, size_x, size_y, size_z = coarse.shape
    expanded = jnp.broadcast_to(
        coarse[:, :, None, :, None, :, None], (components, size_x, 2, size_y, 2, size_z, 2)
    )
    return expanded.reshape(components, 2 * size_x, 2 * size_y, 2 * size_z)


def coarse_update(correction, padded, coarse_rhs, coarse_diag):
    return (
        correction
        + damping
        * (coarse_rhs - (coarse_diag * correction - 0.25 * neighbours(padded)))
        / coarse_diag
    )


def halve_last(values):
    paired = values.reshape(values.shape[:-1] + (values.shape[-1] // 2, 2))
    even_cells = paired[..., 0]
    odd_cells = paired[..., 1]
    return ((even_cells + odd_cells) * root_half, (even_cells - odd_cells) * root_half)


def x_levels(approx):
    details = []
    for level_index in range(LX - 1):
        approx, detail = halve_last(approx)
        details.append(detail)
    return jnp.concatenate([approx] + details[::-1], axis=-1)


def pair_pass(values, which_dim):
    layout = values.shape
    paired = values.reshape(
        layout[:which_dim] + (layout[which_dim] // 2, 2) + layout[which_dim + 1 :]
    )
    even_cells = lax.index_in_dim(paired, 0, which_dim + 1, keepdims=False)
    odd_cells = lax.index_in_dim(paired, 1, which_dim + 1, keepdims=False)
    stacked = jnp.stack(
        [(even_cells + odd_cells) * root_half, (even_cells - odd_cells) * root_half],
        axis=which_dim + 1,
    )
    return stacked.reshape(layout)


def finish_lines(x_lines):
    coeffs = x_levels(x_lines)
    return pair_pass(pair_pass(coeffs, 1), 2)


def on_device(velocity_prev, forcing, reaction):
    components, cells_x, cells_y, cells_z = velocity_prev.shape
    diagonal = (6.0 + reaction)[None]
    depth = SWEEPS + 1
    stacked = jnp.concatenate([velocity_prev, forcing, diagonal], axis=0)
    extended = padded_2(stacked, (("agg", 3), ("gx", 1), ("gy", 2)), depth)
    inside = valid_mask(cells_x, cells_y, cells_z, depth)
    current_ext = extended[:3]
    forcing_ext = extended[3:6]
    diagonal_ext = extended[6:7] * inside + (1.0 - inside)
    for sweep_index in range(SWEEPS + 1):
        shrink = sweep_index + 1
        center = trim_cells(current_ext, 1)
        forcing_in = trim_cells(forcing_ext, shrink)
        diagonal_in = trim_cells(diagonal_ext, shrink)
        residual_in = forcing_in - (diagonal_in * center - neighbours(current_ext))
        if sweep_index < SWEEPS:
            current_ext = center + trim_cells(inside, shrink) * damping * residual_in / diagonal_in
        else:
            current = center
            fine_res = residual_in
    coarse_rhs = block_mean(fine_res)
    coarse_diag = (6.0 + 4.0 * block_mean(reaction[None])) * 0.25
    correction = damping * coarse_rhs / coarse_diag
    for sweep_index in range(COARSE_SWEEPS - 1):
        padded = padded_2(correction, (("agg", 3), ("gx", 1), ("gy", 2)), 1)
        correction = coarse_update(correction, padded, coarse_rhs, coarse_diag)
    current = current + prolong(correction)
    velocity = current + damping * last_residual(current, forcing, diagonal) / diagonal
    x_lines = jnp.transpose(
        lax.all_to_all(velocity_prev, "gx", split_axis=3, concat_axis=1, tiled=True), (0, 2, 3, 1)
    )
    compressed = finish_lines(halve_last(x_lines)[0])
    return (velocity, compressed)


def solution(mesh):
    placed = (P(None, "gx", "gy", "agg"), P(None, "gx", "gy", "agg"), P("gx", "gy", "agg"))
    return jax.shard_map(
        on_device,
        mesh=mesh,
        in_specs=placed,
        out_specs=(P(None, "gx", "gy", "agg"), P(None, "gy", ("agg", "gx"), None)),
        check_vma=False,
    )
```

profile of v0, /device:TPU:1, one launch (start us, length us, event | category | flops | bytes accessed | tf_op | source)
XLA Modules:
  0.0 187.9 jit_solution(10220336205270050194)
XLA Ops:
  0.6 1.5 broadcast_add_fusion
  4.2 4.1 %collective-permute-start = (f32[7,8,16,3]{3,2,1,0:T(8,128)}, f32[7,8,16,3]{3,2,1,0:T(8,128)S(1)}, u32[]{:S(2)}, u32[]{:S(2)}) collective-permute-start(f32[7,8,16,3]{3,2,1,0:T(8,128)} %get-tuple-element.24), channel_id=1, source_target_pairs={{0,16},{1,17},{2,18},{3,19},{4,20},{5,21},{6,22},{7,23},{8,24},{9,... | collective-permute-start | bytes 32264 | tf_op jit(solution)/shard_map/ppermute | solution.py:20
  8.3 1.3 collective-permute-start.1
  11.4 4.3 %all-to-all-start = ((f32[4,1,12288]{2,1,0:T(1,128)}), f32[4,1,12288]{2,1,0:T(1,128)S(1)}, u32[]{:S(2)}, u32[]{:S(2)}) async-start(f32[4,1,12288]{2,1,0:T(1,128)} %reshape.218), calls=%async_computation | async-start | bytes 393216 | tf_op jit(solution)/shard_map/all_to_all | solution.py:145
  15.7 5.6 %reshape_broadcast_in_dim.3 = f32[4,2,8,2,64,2]{5,4,3,2,1,0:T(8,128)} reshape(f32[8,16,128]{2,1,0:T(8,128)S(1)} %copy-done.4) | data formatting | bytes 131072 | tf_op jit(solution)/shard_map/reshape;broadcast_in_dim | solution.py:59
  21.3 2.6 %reduce_sum.19 = f32[4,8,64]{2,1,0:T(8,128)S(1)} reduce(f32[4,2,8,2,64,2]{5,4,3,2,1,0:T(8,128)} %reshape_broadcast_in_dim.3, f32[]{:T(128)} %constant.12.clone.1), dimensions={1,3,5}, to_apply=%region_1.0 | reduce | flops 14336 | bytes 73732 | tf_op jit(solution)/shard_map/reduce_sum | solution.py:59
  24.2 3.5 %collective-permute-start.2 = (f32[7,3,16,134]{3,2,1,0:T(8,128)S(1)}, f32[7,3,16,134]{3,2,1,0:T(8,128)S(1)}, u32[]{:S(2)}, u32[]{:S(2)}) collective-permute-start(f32[7,3,16,134]{3,2,1,0:T(8,128)S(1)} %get-tuple-element.12), channel_id=1, source_target_pairs={{0,4},{4,8},{8,12},{1,5},{5,9},{9,13},{2,6},{6,10},{10,14},{3,7},{... | collective-permute-start | bytes 540296 | tf_op jit(solution)/shard_map/ppermute | solution.py:20
  27.8 1.9 %collective-permute-start.3 = (f32[7,3,16,134]{3,2,1,0:T(8,128)S(1)}, f32[7,3,16,134]{3,2,1,0:T(8,128)S(1)}, u32[]{:S(2)}, u32[]{:S(2)}) collective-permute-start(f32[7,3,16,134]{3,2,1,0:T(8,128)S(1)} %get-tuple-element.13), channel_id=1, source_target_pairs={{4,0},{8,4},{12,8},{5,1},{9,5},{13,9},{6,2},{10,6},{14,10},{7,3},{... | collective-permute-start | bytes 540296 | tf_op jit(solution)/shard_map/ppermute | solution.py:23
  29.7 2.2 %collective-permute-done.2 = f32[7,3,16,134]{3,2,1,0:T(8,128)S(1)} collective-permute-done((f32[7,3,16,134]{3,2,1,0:T(8,128)S(1)}, f32[7,3,16,134]{3,2,1,0:T(8,128)S(1)}, u32[]{:S(2)}, u32[]{:S(2)}) %collective-permute-start.2) | collective-permute-done | bytes 180128 | tf_op jit(solution)/shard_map/ppermute | solution.py:20
  32.0 4.4 %collective-permute-done.3 = f32[7,3,16,134]{3,2,1,0:T(8,128)S(1)} collective-permute-done((f32[7,3,16,134]{3,2,1,0:T(8,128)S(1)}, f32[7,3,16,134]{3,2,1,0:T(8,128)S(1)}, u32[]{:S(2)}, u32[]{:S(2)}) %collective-permute-start.3) | collective-permute-done | bytes 180128 | tf_op jit(solution)/shard_map/ppermute | solution.py:23
  37.5 3.2 %collective-permute-start.4 = (f32[7,14,3,134]{3,2,1,0:T(4,128)}, f32[7,14,3,134]{3,2,1,0:T(4,128)S(1)}, u32[]{:S(2)}, u32[]{:S(2)}) collective-permute-start(f32[7,14,3,134]{3,2,1,0:T(4,128)} %get-tuple-element.8), channel_id=1, source_target_pairs={{0,1},{1,2},{2,3},{4,5},{5,6},{6,7},{8,9},{9,10},{10,11},{12,13},{... | collective-permute-start | bytes 472760 | tf_op jit(solution)/shard_map/ppermute | solution.py:20
  40.8 1.3 collective-permute-start.5
  42.1 3.7 %collective-permute-done.4 = f32[7,14,3,134]{3,2,1,0:T(4,128)S(1)} collective-permute-done((f32[7,14,3,134]{3,2,1,0:T(4,128)}, f32[7,14,3,134]{3,2,1,0:T(4,128)S(1)}, u32[]{:S(2)}, u32[]{:S(2)}) %collective-permute-start.4) | collective-permute-done | bytes 157616 | tf_op jit(solution)/shard_map/ppermute | solution.py:20
  45.8 3.6 %collective-permute-done.5 = f32[7,14,3,134]{3,2,1,0:T(4,128)S(1)} collective-permute-done((f32[7,14,3,134]{3,2,1,0:T(4,128)S(1)}, f32[7,14,3,134]{3,2,1,0:T(4,128)S(1)}, u32[]{:S(2)}, u32[]{:S(2)}) %collective-permute-start.5) | collective-permute-done | bytes 157616 | tf_op jit(solution)/shard_map/ppermute | solution.py:23
  50.8 1.7 fusion.4
  52.4 1.4 fusion.9
  54.2 14.0 %reshape.214 = f32[3,4,2,8,2,64,2]{6,5,4,3,2,1,0:T(8,128)} reshape(f32[3,8,16,128]{3,2,1,0:T(8,128)S(1)} %fusion.26) | data formatting | bytes 393216 | tf_op jit(solution)/shard_map/reshape | solution.py:59
  68.2 5.5 %reduce_sum.18 = f32[3,4,8,64]{3,2,1,0:T(8,128)S(1)} reduce(f32[3,4,2,8,2,64,2]{6,5,4,3,2,1,0:T(8,128)} %reshape.214, f32[]{:T(128)} %constant.12.clone.1), dimensions={2,4,6}, to_apply=%region_0.0 | reduce | flops 43008 | bytes 221188 | tf_op jit(solution)/shard_map/reduce_sum | solution.py:59
  73.8 4.3 %collective-permute-start.6 = (f32[3,4,8,1]{3,2,1,0:T(8,128)S(1)}, f32[3,4,8,1]{3,2,1,0:T(8,128)S(1)}, u32[]{:S(2)}, u32[]{:S(2)}) collective-permute-start(f32[3,4,8,1]{3,2,1,0:T(8,128)S(1)} %get-tuple-element.53), channel_id=1, source_target_pairs={{0,16},{1,17},{2,18},{3,19},{4,20},{5,21},{6,22},{7,23},{8,24},{9,... | collective-permute-start | bytes 1160 | tf_op jit(solution)/shard_map/ppermute | solution.py:20
  78.1 1.3 collective-permute-start.7
  79.5 3.5 %collective-permute-done.7 = f32[3,4,8,1]{3,2,1,0:T(8,128)S(1)} collective-permute-done((f32[3,4,8,1]{3,2,1,0:T(8,128)S(1)}, f32[3,4,8,1]{3,2,1,0:T(8,128)S(1)}, u32[]{:S(2)}, u32[]{:S(2)}) %collective-permute-start.7) | collective-permute-done | bytes 416 | tf_op jit(solution)/shard_map/ppermute | solution.py:23
  83.1 1.9 %collective-permute-start.8 = (f32[3,1,8,66]{3,2,1,0:T(8,128)S(1)}, f32[3,1,8,66]{3,2,1,0:T(8,128)S(1)}, u32[]{:S(2)}, u32[]{:S(2)}) collective-permute-start(f32[3,1,8,66]{3,2,1,0:T(8,128)S(1)} %get-tuple-element.43), channel_id=1, source_target_pairs={{4,0},{8,4},{12,8},{5,1},{9,5},{13,9},{6,2},{10,6},{14,10},{7,3},{... | collective-permute-start | bytes 19016 | tf_op jit(solution)/shard_map/ppermute | solution.py:23
  85.0 4.8 %collective-permute-start.9 = (f32[3,1,8,66]{3,2,1,0:T(8,128)S(1)}, f32[3,1,8,66]{3,2,1,0:T(8,128)S(1)}, u32[]{:S(2)}, u32[]{:S(2)}) collective-permute-start(f32[3,1,8,66]{3,2,1,0:T(8,128)S(1)} %get-tuple-element.42), channel_id=1, source_target_pairs={{0,4},{4,8},{8,12},{1,5},{5,9},{9,13},{2,6},{6,10},{10,14},{3,7},{... | collective-permute-start | bytes 19016 | tf_op jit(solution)/shard_map/ppermute | solution.py:20
  92.7 1.3 collective-permute-start.10
  94.0 4.0 %collective-permute-start.11 = (f32[3,6,1,66]{3,2,1,0:T(1,128)S(1)}, f32[3,6,1,66]{3,2,1,0:T(1,128)S(1)}, u32[]{:S(2)}, u32[]{:S(2)}) collective-permute-start(f32[3,6,1,66]{3,2,1,0:T(1,128)S(1)} %get-tuple-element.37), channel_id=1, source_target_pairs={{0,1},{1,2},{2,3},{4,5},{5,6},{6,7},{8,9},{9,10},{10,11},{12,13},{... | collective-permute-start | bytes 14264 | tf_op jit(solution)/shard_map/ppermute | solution.py:20
  99.1 1.3 collective-permute-start.12
  100.4 1.3 collective-permute-start.13
  102.4 3.6 %collective-permute-done.13 = f32[3,4,8,1]{3,2,1,0:T(8,128)S(1)} collective-permute-done((f32[3,4,8,1]{3,2,1,0:T(8,128)S(1)}, f32[3,4,8,1]{3,2,1,0:T(8,128)S(1)}, u32[]{:S(2)}, u32[]{:S(2)}) %collective-permute-start.13) | collective-permute-done | bytes 416 | tf_op jit(solution)/shard_map/ppermute | solution.py:23
  106.2 2.3 %collective-permute-start.14 = (f32[3,1,8,66]{3,2,1,0:T(8,128)S(1)}, f32[3,1,8,66]{3,2,1,0:T(8,128)S(1)}, u32[]{:S(2)}, u32[]{:S(2)}) collective-permute-start(f32[3,1,8,66]{3,2,1,0:T(8,128)S(1)} %get-tuple-element.41), channel_id=1, source_target_pairs={{4,0},{8,4},{12,8},{5,1},{9,5},{13,9},{6,2},{10,6},{14,10},{7,3},{... | collective-permute-start | bytes 19016 | tf_op jit(solution)/shard_map/ppermute | solution.py:23
  108.5 3.8 %collective-permute-start.15 = (f32[3,1,8,66]{3,2,1,0:T(8,128)S(1)}, f32[3,1,8,66]{3,2,1,0:T(8,128)S(1)}, u32[]{:S(2)}, u32[]{:S(2)}) collective-permute-start(f32[3,1,8,66]{3,2,1,0:T(8,128)S(1)} %get-tuple-element.40), channel_id=1, source_target_pairs={{0,4},{4,8},{8,12},{1,5},{5,9},{9,13},{2,6},{6,10},{10,14},{3,7},{... | collective-permute-start | bytes 19016 | tf_op jit(solution)/shard_map/ppermute | solution.py:20
  113.2 1.3 collective-permute-start.16
  114.5 4.5 %collective-permute-start.17 = (f32[3,6,1,66]{3,2,1,0:T(1,128)S(1)}, f32[3,6,1,66]{3,2,1,0:T(1,128)S(1)}, u32[]{:S(2)}, u32[]{:S(2)}) collective-permute-start(f32[3,6,1,66]{3,2,1,0:T(1,128)S(1)} %get-tuple-element.35), channel_id=1, source_target_pairs={{0,1},{1,2},{2,3},{4,5},{5,6},{6,7},{8,9},{9,10},{10,11},{12,13},{... | collective-permute-start | bytes 14264 | tf_op jit(solution)/shard_map/ppermute | solution.py:20
  120.1 1.3 collective-permute-start.18
  121.4 1.3 collective-permute-start.19
  123.0 3.8 %collective-permute-done.19 = f32[3,4,8,1]{3,2,1,0:T(8,128)S(1)} collective-permute-done((f32[3,4,8,1]{3,2,1,0:T(8,128)S(1)}, f32[3,4,8,1]{3,2,1,0:T(8,128)S(1)}, u32[]{:S(2)}, u32[]{:S(2)}) %collective-permute-start.19) | collective-permute-done | bytes 416 | tf_op jit(solution)/shard_map/ppermute | solution.py:23
  126.9 2.3 %collective-permute-start.20 = (f32[3,1,8,66]{3,2,1,0:T(8,128)S(1)}, f32[3,1,8,66]{3,2,1,0:T(8,128)S(1)}, u32[]{:S(2)}, u32[]{:S(2)}) collective-permute-start(f32[3,1,8,66]{3,2,1,0:T(8,128)S(1)} %get-tuple-element.39), channel_id=1, source_target_pairs={{4,0},{8,4},{12,8},{5,1},{9,5},{13,9},{6,2},{10,6},{14,10},{7,3},{... | collective-permute-start | bytes 19016 | tf_op jit(solution)/shard_map/ppermute | solution.py:23
  129.2 5.6 %collective-permute-start.21 = (f32[3,1,8,66]{3,2,1,0:T(8,128)S(1)}, f32[3,1,8,66]{3,2,1,0:T(8,128)S(1)}, u32[]{:S(2)}, u32[]{:S(2)}) collective-permute-start(f32[3,1,8,66]{3,2,1,0:T(8,128)S(1)} %get-tuple-element.38), channel_id=1, source_target_pairs={{0,4},{4,8},{8,12},{1,5},{5,9},{9,13},{2,6},{6,10},{10,14},{3,7},{... | collective-permute-start | bytes 19016 | tf_op jit(solution)/shard_map/ppermute | solution.py:20
  134.8 1.5 subtract_multiply_fusion.1
  137.8 3.0 %concatenate.152 = f32[3,8,2,32,16]{4,3,2,1,0:T(8,128)S(1)} concatenate(f32[3,8,2,32,1]{4,3,2,1,0:T(8,128)} %bitcast.54, f32[3,8,2,32,1]{4,3,2,1,0:T(8,128)} %bitcast.53, f32[3,8,2,32,2]{4,3,2,1,0:T(8,128)S(1)} %bitcast.50, f32[3,8,2,32,4]{4,3,2,1,0:T(8,128)S(1)} %bitcast.49, f32[3,8,2,32,8]{4,3,2,1,0:T(8,128)} %copy.34), dimensions={4} | concatenate | bytes 196608 | tf_op jit(solution)/shard_map/concatenate | solution.py:93
  142.3 4.5 %collective-permute-start.23 = (f32[3,6,1,66]{3,2,1,0:T(1,128)S(1)}, f32[3,6,1,66]{3,2,1,0:T(1,128)S(1)}, u32[]{:S(2)}, u32[]{:S(2)}) collective-permute-start(f32[3,6,1,66]{3,2,1,0:T(1,128)S(1)} %get-tuple-element.33), channel_id=1, source_target_pairs={{0,1},{1,2},{2,3},{4,5},{5,6},{6,7},{8,9},{9,10},{10,11},{12,13},{... | collective-permute-start | bytes 14264 | tf_op jit(solution)/shard_map/ppermute | solution.py:20
  147.8 5.3 %broadcast_in_dim.5 = f32[3,4,2,8,2,64,2]{6,5,4,3,2,1,0:T(8,128)} broadcast(f32[3,4,8,64]{3,2,1,0:T(8,128)S(1)} %fusion.33), dimensions={0,1,3,5} | broadcast | bytes 221184 | tf_op jit(solution)/shard_map/broadcast_in_dim | solution.py:66
  153.1 9.8 %reshape.215 = f32[3,8,16,128]{3,2,1,0:T(8,128)S(1)} reshape(f32[3,4,2,8,2,64,2]{6,5,4,3,2,1,0:T(8,128)} %broadcast_in_dim.5) | data formatting | bytes 393216 | tf_op jit(solution)/shard_map/reshape | solution.py:69
  163.1 1.3 collective-permute-start.24
  165.8 1.3 collective-permute-done.24
  167.1 4.1 %collective-permute-done.25 = f32[3,8,16,1]{3,2,1,0:T(8,128)S(1)} collective-permute-done((f32[3,8,16,1]{3,2,1,0:T(8,128)S(1)}, f32[3,8,16,1]{3,2,1,0:T(8,128)S(1)}, u32[]{:S(2)}, u32[]{:S(2)}) %collective-permute-start.25) | collective-permute-done | bytes 1568 | tf_op jit(solution)/shard_map/ppermute | solution.py:23
  171.3 1.9 %collective-permute-start.26 = (f32[3,1,16,130]{3,2,1,0:T(8,128)S(1)}, f32[3,1,16,130]{3,2,1,0:T(8,128)S(1)}, u32[]{:S(2)}, u32[]{:S(2)}) collective-permute-start(f32[3,1,16,130]{3,2,1,0:T(8,128)S(1)} %get-tuple-element.23), channel_id=1, source_target_pairs={{4,0},{8,4},{12,8},{5,1},{9,5},{13,9},{6,2},{10,6},{14,10},{7,3},{... | collective-permute-start | bytes 74888 | tf_op jit(solution)/shard_map/ppermute | solution.py:23
  173.3 4.3 %collective-permute-start.27 = (f32[3,1,16,130]{3,2,1,0:T(8,128)S(1)}, f32[3,1,16,130]{3,2,1,0:T(8,128)S(1)}, u32[]{:S(2)}, u32[]{:S(2)}) collective-permute-start(f32[3,1,16,130]{3,2,1,0:T(8,128)S(1)} %get-tuple-element.22), channel_id=1, source_target_pairs={{0,4},{4,8},{8,12},{1,5},{5,9},{9,13},{2,6},{6,10},{10,14},{3,7},{... | collective-permute-start | bytes 74888 | tf_op jit(solution)/shard_map/ppermute | solution.py:20
  180.2 4.5 %collective-permute-start.29 = (f32[3,10,1,130]{3,2,1,0:T(1,128)S(1)}, f32[3,10,1,130]{3,2,1,0:T(1,128)S(1)}, u32[]{:S(2)}, u32[]{:S(2)}) collective-permute-start(f32[3,10,1,130]{3,2,1,0:T(1,128)S(1)} %get-tuple-element.21), channel_id=1, source_target_pairs={{0,1},{1,2},{2,3},{4,5},{5,6},{6,7},{8,9},{9,10},{10,11},{12,13},{... | collective-permute-start | bytes 46808 | tf_op jit(solution)/shard_map/ppermute | solution.py:20
  (91 shorter events, 25.8 us)
Async XLA Ops:
  0.6 9.0 %copy-start.1 = (f32[3,8,16,128]{3,2,1,0:T(8,128)S(1)}, f32[3,8,16,128]{3,2,1,0:T(8,128)}, u32[]{:S(2)}) copy-start(f32[3,8,16,128]{3,2,1,0:T(8,128)} %param.3) | copy-start | bytes 589828
  4.2 11.5 %copy-start.4 = (f32[8,16,128]{2,1,0:T(8,128)S(1)}, f32[8,16,128]{2,1,0:T(8,128)}, u32[]{:S(2)}) copy-start(f32[8,16,128]{2,1,0:T(8,128)} %param.5) | copy-start | bytes 196612
  4.2 19.7 %collective-permute-start = (f32[7,8,16,3]{3,2,1,0:T(8,128)}, f32[7,8,16,3]{3,2,1,0:T(8,128)S(1)}, u32[]{:S(2)}, u32[]{:S(2)}) collective-permute-start(f32[7,8,16,3]{3,2,1,0:T(8,128)} %get-tuple-element.24), channel_id=1, source_target_pairs={{0,16},{1,17},{2,18},{3,19},{4,20},{5,21},{6,22},{7,23},{8,24},{9,... | collective-permute-start | bytes 32264 | tf_op jit(solution)/shard_map/ppermute | solution.py:20
  8.3 15.6 %collective-permute-start.1 = (f32[7,8,16,3]{3,2,1,0:T(8,128)S(1)}, f32[7,8,16,3]{3,2,1,0:T(8,128)S(1)}, u32[]{:S(2)}, u32[]{:S(2)}) collective-permute-start(f32[7,8,16,3]{3,2,1,0:T(8,128)S(1)} %get-tuple-element.25), channel_id=1, source_target_pairs={{16,0},{17,1},{18,2},{19,3},{20,4},{21,5},{22,6},{23,7},{24,8},{25... | collective-permute-start | bytes 32264 | tf_op jit(solution)/shard_map/ppermute | solution.py:23
  11.4 78.3 %all-to-all-start = ((f32[4,1,12288]{2,1,0:T(1,128)}), f32[4,1,12288]{2,1,0:T(1,128)S(1)}, u32[]{:S(2)}, u32[]{:S(2)}) async-start(f32[4,1,12288]{2,1,0:T(1,128)} %reshape.218), calls=%async_computation | async-start | bytes 393216 | tf_op jit(solution)/shard_map/all_to_all | solution.py:145
  21.3 2.6 %copy-start = (f32[3,8,16,128]{3,2,1,0:T(8,128)S(1)}, f32[3,8,16,128]{3,2,1,0:T(8,128)}, u32[]{:S(2)}) copy-start(f32[3,8,16,128]{3,2,1,0:T(8,128)} %param.4) | copy-start | bytes 589828
  24.2 7.7 %collective-permute-start.2 = (f32[7,3,16,134]{3,2,1,0:T(8,128)S(1)}, f32[7,3,16,134]{3,2,1,0:T(8,128)S(1)}, u32[]{:S(2)}, u32[]{:S(2)}) collective-permute-start(f32[7,3,16,134]{3,2,1,0:T(8,128)S(1)} %get-tuple-element.12), channel_id=1, source_target_pairs={{0,4},{4,8},{8,12},{1,5},{5,9},{9,13},{2,6},{6,10},{10,14},{3,7},{... | collective-permute-start | bytes 540296 | tf_op jit(solution)/shard_map/ppermute | solution.py:20
  27.8 8.6 %collective-permute-start.3 = (f32[7,3,16,134]{3,2,1,0:T(8,128)S(1)}, f32[7,3,16,134]{3,2,1,0:T(8,128)S(1)}, u32[]{:S(2)}, u32[]{:S(2)}) collective-permute-start(f32[7,3,16,134]{3,2,1,0:T(8,128)S(1)} %get-tuple-element.13), channel_id=1, source_target_pairs={{4,0},{8,4},{12,8},{5,1},{9,5},{13,9},{6,2},{10,6},{14,10},{7,3},{... | collective-permute-start | bytes 540296 | tf_op jit(solution)/shard_map/ppermute | solution.py:23
  37.5 8.3 %collective-permute-start.4 = (f32[7,14,3,134]{3,2,1,0:T(4,128)}, f32[7,14,3,134]{3,2,1,0:T(4,128)S(1)}, u32[]{:S(2)}, u32[]{:S(2)}) collective-permute-start(f32[7,14,3,134]{3,2,1,0:T(4,128)} %get-tuple-element.8), channel_id=1, source_target_pairs={{0,1},{1,2},{2,3},{4,5},{5,6},{6,7},{8,9},{9,10},{10,11},{12,13},{... | collective-permute-start | bytes 472760 | tf_op jit(solution)/shard_map/ppermute | solution.py:20
  40.8 8.6 %collective-permute-start.5 = (f32[7,14,3,134]{3,2,1,0:T(4,128)S(1)}, f32[7,14,3,134]{3,2,1,0:T(4,128)S(1)}, u32[]{:S(2)}, u32[]{:S(2)}) collective-permute-start(f32[7,14,3,134]{3,2,1,0:T(4,128)S(1)} %get-tuple-element.9), channel_id=1, source_target_pairs={{1,0},{2,1},{3,2},{5,4},{6,5},{7,6},{9,8},{10,9},{11,10},{13,12},{... | collective-permute-start | bytes 472760 | tf_op jit(solution)/shard_map/ppermute | solution.py:23
  73.8 5.6 %collective-permute-start.6 = (f32[3,4,8,1]{3,2,1,0:T(8,128)S(1)}, f32[3,4,8,1]{3,2,1,0:T(8,128)S(1)}, u32[]{:S(2)}, u32[]{:S(2)}) collective-permute-start(f32[3,4,8,1]{3,2,1,0:T(8,128)S(1)} %get-tuple-element.53), channel_id=1, source_target_pairs={{0,16},{1,17},{2,18},{3,19},{4,20},{5,21},{6,22},{7,23},{8,24},{9,... | collective-permute-start | bytes 1160 | tf_op jit(solution)/shard_map/ppermute | solution.py:20
  78.1 4.8 %collective-permute-start.7 = (f32[3,4,8,1]{3,2,1,0:T(8,128)S(1)}, f32[3,4,8,1]{3,2,1,0:T(8,128)S(1)}, u32[]{:S(2)}, u32[]{:S(2)}) collective-permute-start(f32[3,4,8,1]{3,2,1,0:T(8,128)S(1)} %get-tuple-element.52), channel_id=1, source_target_pairs={{16,0},{17,1},{18,2},{19,3},{20,4},{21,5},{22,6},{23,7},{24,8},{25... | collective-permute-start | bytes 1160 | tf_op jit(solution)/shard_map/ppermute | solution.py:23
  83.1 9.5 %collective-permute-start.8 = (f32[3,1,8,66]{3,2,1,0:T(8,128)S(1)}, f32[3,1,8,66]{3,2,1,0:T(8,128)S(1)}, u32[]{:S(2)}, u32[]{:S(2)}) collective-permute-start(f32[3,1,8,66]{3,2,1,0:T(8,128)S(1)} %get-tuple-element.43), channel_id=1, source_target_pairs={{4,0},{8,4},{12,8},{5,1},{9,5},{13,9},{6,2},{10,6},{14,10},{7,3},{... | collective-permute-start | bytes 19016 | tf_op jit(solution)/shard_map/ppermute | solution.py:23
  85.0 7.6 %collective-permute-start.9 = (f32[3,1,8,66]{3,2,1,0:T(8,128)S(1)}, f32[3,1,8,66]{3,2,1,0:T(8,128)S(1)}, u32[]{:S(2)}, u32[]{:S(2)}) collective-permute-start(f32[3,1,8,66]{3,2,1,0:T(8,128)S(1)} %get-tuple-element.42), channel_id=1, source_target_pairs={{0,4},{4,8},{8,12},{1,5},{5,9},{9,13},{2,6},{6,10},{10,14},{3,7},{... | collective-permute-start | bytes 19016 | tf_op jit(solution)/shard_map/ppermute | solution.py:20
  92.7 5.4 %collective-permute-start.10 = (f32[3,6,1,66]{3,2,1,0:T(1,128)S(1)}, f32[3,6,1,66]{3,2,1,0:T(1,128)S(1)}, u32[]{:S(2)}, u32[]{:S(2)}) collective-permute-start(f32[3,6,1,66]{3,2,1,0:T(1,128)S(1)} %get-tuple-element.36), channel_id=1, source_target_pairs={{1,0},{2,1},{3,2},{5,4},{6,5},{7,6},{9,8},{10,9},{11,10},{13,12},{... | collective-permute-start | bytes 14264 | tf_op jit(solution)/shard_map/ppermute | solution.py:23
  94.0 4.8 %collective-permute-start.11 = (f32[3,6,1,66]{3,2,1,0:T(1,128)S(1)}, f32[3,6,1,66]{3,2,1,0:T(1,128)S(1)}, u32[]{:S(2)}, u32[]{:S(2)}) collective-permute-start(f32[3,6,1,66]{3,2,1,0:T(1,128)S(1)} %get-tuple-element.37), channel_id=1, source_target_pairs={{0,1},{1,2},{2,3},{4,5},{5,6},{6,7},{8,9},{9,10},{10,11},{12,13},{... | collective-permute-start | bytes 14264 | tf_op jit(solution)/shard_map/ppermute | solution.py:20
  99.1 3.3 %collective-permute-start.12 = (f32[3,4,8,1]{3,2,1,0:T(8,128)S(1)}, f32[3,4,8,1]{3,2,1,0:T(8,128)S(1)}, u32[]{:S(2)}, u32[]{:S(2)}) collective-permute-start(f32[3,4,8,1]{3,2,1,0:T(8,128)S(1)} %get-tuple-element.51), channel_id=1, source_target_pairs={{0,16},{1,17},{2,18},{3,19},{4,20},{5,21},{6,22},{7,23},{8,24},{9,... | collective-permute-start | bytes 1160 | tf_op jit(solution)/shard_map/ppermute | solution.py:20
  100.4 5.6 %collective-permute-start.13 = (f32[3,4,8,1]{3,2,1,0:T(8,128)S(1)}, f32[3,4,8,1]{3,2,1,0:T(8,128)S(1)}, u32[]{:S(2)}, u32[]{:S(2)}) collective-permute-start(f32[3,4,8,1]{3,2,1,0:T(8,128)S(1)} %get-tuple-element.50), channel_id=1, source_target_pairs={{16,0},{17,1},{18,2},{19,3},{20,4},{21,5},{22,6},{23,7},{24,8},{25... | collective-permute-start | bytes 1160 | tf_op jit(solution)/shard_map/ppermute | solution.py:23
  106.2 6.8 %collective-permute-start.14 = (f32[3,1,8,66]{3,2,1,0:T(8,128)S(1)}, f32[3,1,8,66]{3,2,1,0:T(8,128)S(1)}, u32[]{:S(2)}, u32[]{:S(2)}) collective-permute-start(f32[3,1,8,66]{3,2,1,0:T(8,128)S(1)} %get-tuple-element.41), channel_id=1, source_target_pairs={{4,0},{8,4},{12,8},{5,1},{9,5},{13,9},{6,2},{10,6},{14,10},{7,3},{... | collective-permute-start | bytes 19016 | tf_op jit(solution)/shard_map/ppermute | solution.py:23
  108.5 4.6 %collective-permute-start.15 = (f32[3,1,8,66]{3,2,1,0:T(8,128)S(1)}, f32[3,1,8,66]{3,2,1,0:T(8,128)S(1)}, u32[]{:S(2)}, u32[]{:S(2)}) collective-permute-start(f32[3,1,8,66]{3,2,1,0:T(8,128)S(1)} %get-tuple-element.40), channel_id=1, source_target_pairs={{0,4},{4,8},{8,12},{1,5},{5,9},{9,13},{2,6},{6,10},{10,14},{3,7},{... | collective-permute-start | bytes 19016 | tf_op jit(solution)/shard_map/ppermute | solution.py:20
  113.2 6.6 %collective-permute-start.16 = (f32[3,6,1,66]{3,2,1,0:T(1,128)S(1)}, f32[3,6,1,66]{3,2,1,0:T(1,128)S(1)}, u32[]{:S(2)}, u32[]{:S(2)}) collective-permute-start(f32[3,6,1,66]{3,2,1,0:T(1,128)S(1)} %get-tuple-element.34), channel_id=1, source_target_pairs={{1,0},{2,1},{3,2},{5,4},{6,5},{7,6},{9,8},{10,9},{11,10},{13,12},{... | collective-permute-start | bytes 14264 | tf_op jit(solution)/shard_map/ppermute | solution.py:23
  114.5 5.3 %collective-permute-start.17 = (f32[3,6,1,66]{3,2,1,0:T(1,128)S(1)}, f32[3,6,1,66]{3,2,1,0:T(1,128)S(1)}, u32[]{:S(2)}, u32[]{:S(2)}) collective-permute-start(f32[3,6,1,66]{3,2,1,0:T(1,128)S(1)} %get-tuple-element.35), channel_id=1, source_target_pairs={{0,1},{1,2},{2,3},{4,5},{5,6},{6,7},{8,9},{9,10},{10,11},{12,13},{... | collective-permute-start | bytes 14264 | tf_op jit(solution)/shard_map/ppermute | solution.py:20
  120.1 2.9 %collective-permute-start.18 = (f32[3,4,8,1]{3,2,1,0:T(8,128)S(1)}, f32[3,4,8,1]{3,2,1,0:T(8,128)S(1)}, u32[]{:S(2)}, u32[]{:S(2)}) collective-permute-start(f32[3,4,8,1]{3,2,1,0:T(8,128)S(1)} %get-tuple-element.49), channel_id=1, source_target_pairs={{0,16},{1,17},{2,18},{3,19},{4,20},{5,21},{6,22},{7,23},{8,24},{9,... | collective-permute-start | bytes 1160 | tf_op jit(solution)/shard_map/ppermute | solution.py:20
  121.4 5.3 %collective-permute-start.19 = (f32[3,4,8,1]{3,2,1,0:T(8,128)S(1)}, f32[3,4,8,1]{3,2,1,0:T(8,128)S(1)}, u32[]{:S(2)}, u32[]{:S(2)}) collective-permute-start(f32[3,4,8,1]{3,2,1,0:T(8,128)S(1)} %get-tuple-element.48), channel_id=1, source_target_pairs={{16,0},{17,1},{18,2},{19,3},{20,4},{21,5},{22,6},{23,7},{24,8},{25... | collective-permute-start | bytes 1160 | tf_op jit(solution)/shard_map/ppermute | solution.py:23
  123.0 13.3 %copy-start.3 = (f32[3,16,32,4,1]{2,1,4,3,0:T(8,128)S(1)}, f32[3,16,32,4,1]{2,1,4,3,0:T(8,128)}, u32[]{:S(2)}) copy-start(f32[3,16,32,4,1]{2,1,4,3,0:T(8,128)} %get-tuple-element.28) | copy-start | bytes 73732
  123.0 13.6 %copy-start.2 = (f32[3,16,32,8,1]{2,1,4,3,0:T(8,128)S(1)}, f32[3,16,32,8,1]{2,1,4,3,0:T(8,128)}, u32[]{:S(2)}) copy-start(f32[3,16,32,8,1]{2,1,4,3,0:T(8,128)} %get-tuple-element.26) | copy-start | bytes 147460
  126.9 14.0 %collective-permute-start.20 = (f32[3,1,8,66]{3,2,1,0:T(8,128)S(1)}, f32[3,1,8,66]{3,2,1,0:T(8,128)S(1)}, u32[]{:S(2)}, u32[]{:S(2)}) collective-permute-start(f32[3,1,8,66]{3,2,1,0:T(8,128)S(1)} %get-tuple-element.39), channel_id=1, source_target_pairs={{4,0},{8,4},{12,8},{5,1},{9,5},{13,9},{6,2},{10,6},{14,10},{7,3},{... | collective-permute-start | bytes 19016 | tf_op jit(solution)/shard_map/ppermute | solution.py:23
  129.2 11.7 %collective-permute-start.21 = (f32[3,1,8,66]{3,2,1,0:T(8,128)S(1)}, f32[3,1,8,66]{3,2,1,0:T(8,128)S(1)}, u32[]{:S(2)}, u32[]{:S(2)}) collective-permute-start(f32[3,1,8,66]{3,2,1,0:T(8,128)S(1)} %get-tuple-element.38), channel_id=1, source_target_pairs={{0,4},{4,8},{8,12},{1,5},{5,9},{9,13},{2,6},{6,10},{10,14},{3,7},{... | collective-permute-start | bytes 19016 | tf_op jit(solution)/shard_map/ppermute | solution.py:20
  141.0 6.0 %collective-permute-start.22 = (f32[3,6,1,66]{3,2,1,0:T(1,128)S(1)}, f32[3,6,1,66]{3,2,1,0:T(1,128)S(1)}, u32[]{:S(2)}, u32[]{:S(2)}) collective-permute-start(f32[3,6,1,66]{3,2,1,0:T(1,128)S(1)} %get-tuple-element.32), channel_id=1, source_target_pairs={{1,0},{2,1},{3,2},{5,4},{6,5},{7,6},{9,8},{10,9},{11,10},{13,12},{... | collective-permute-start | bytes 14264 | tf_op jit(solution)/shard_map/ppermute | solution.py:23
  142.3 5.3 %collective-permute-start.23 = (f32[3,6,1,66]{3,2,1,0:T(1,128)S(1)}, f32[3,6,1,66]{3,2,1,0:T(1,128)S(1)}, u32[]{:S(2)}, u32[]{:S(2)}) collective-permute-start(f32[3,6,1,66]{3,2,1,0:T(1,128)S(1)} %get-tuple-element.33), channel_id=1, source_target_pairs={{0,1},{1,2},{2,3},{4,5},{5,6},{6,7},{8,9},{9,10},{10,11},{12,13},{... | collective-permute-start | bytes 14264 | tf_op jit(solution)/shard_map/ppermute | solution.py:20
  163.1 4.0 %collective-permute-start.24 = (f32[3,8,16,1]{3,2,1,0:T(8,128)S(1)}, f32[3,8,16,1]{3,2,1,0:T(8,128)S(1)}, u32[]{:S(2)}, u32[]{:S(2)}) collective-permute-start(f32[3,8,16,1]{3,2,1,0:T(8,128)S(1)} %get-tuple-element.31), channel_id=1, source_target_pairs={{0,16},{1,17},{2,18},{3,19},{4,20},{5,21},{6,22},{7,23},{8,24},{9,... | collective-permute-start | bytes 4616 | tf_op jit(solution)/shard_map/ppermute | solution.py:20
  164.4 6.8 %collective-permute-start.25 = (f32[3,8,16,1]{3,2,1,0:T(8,128)S(1)}, f32[3,8,16,1]{3,2,1,0:T(8,128)S(1)}, u32[]{:S(2)}, u32[]{:S(2)}) collective-permute-start(f32[3,8,16,1]{3,2,1,0:T(8,128)S(1)} %get-tuple-element.30), channel_id=1, source_target_pairs={{16,0},{17,1},{18,2},{19,3},{20,4},{21,5},{22,6},{23,7},{24,8},{25... | collective-permute-start | bytes 4616 | tf_op jit(solution)/shard_map/ppermute | solution.py:23
  171.3 7.1 %collective-permute-start.26 = (f32[3,1,16,130]{3,2,1,0:T(8,128)S(1)}, f32[3,1,16,130]{3,2,1,0:T(8,128)S(1)}, u32[]{:S(2)}, u32[]{:S(2)}) collective-permute-start(f32[3,1,16,130]{3,2,1,0:T(8,128)S(1)} %get-tuple-element.23), channel_id=1, source_target_pairs={{4,0},{8,4},{12,8},{5,1},{9,5},{13,9},{6,2},{10,6},{14,10},{7,3},{... | collective-permute-start | bytes 74888 | tf_op jit(solution)/shard_map/ppermute | solution.py:23
  173.3 5.4 %collective-permute-start.27 = (f32[3,1,16,130]{3,2,1,0:T(8,128)S(1)}, f32[3,1,16,130]{3,2,1,0:T(8,128)S(1)}, u32[]{:S(2)}, u32[]{:S(2)}) collective-permute-start(f32[3,1,16,130]{3,2,1,0:T(8,128)S(1)} %get-tuple-element.22), channel_id=1, source_target_pairs={{0,4},{4,8},{8,12},{1,5},{5,9},{9,13},{2,6},{6,10},{10,14},{3,7},{... | collective-permute-start | bytes 74888 | tf_op jit(solution)/shard_map/ppermute | solution.py:20
  177.6 9.1 %copy-start.5 = (f32[8,16,128]{2,1,0:T(8,128)S(1)}, f32[8,16,128]{2,1,0:T(8,128)}, u32[]{:S(2)}) copy-start(f32[8,16,128]{2,1,0:T(8,128)} %get-tuple-element.46) | copy-start | bytes 196612
  178.9 7.8 %collective-permute-start.28 = (f32[3,10,1,130]{3,2,1,0:T(1,128)S(1)}, f32[3,10,1,130]{3,2,1,0:T(1,128)S(1)}, u32[]{:S(2)}, u32[]{:S(2)}) collective-permute-start(f32[3,10,1,130]{3,2,1,0:T(1,128)S(1)} %get-tuple-element.20), channel_id=1, source_target_pairs={{1,0},{2,1},{3,2},{5,4},{6,5},{7,6},{9,8},{10,9},{11,10},{13,12},{... | collective-permute-start | bytes 46808 | tf_op jit(solution)/shard_map/ppermute | solution.py:23
  180.2 6.5 %collective-permute-start.29 = (f32[3,10,1,130]{3,2,1,0:T(1,128)S(1)}, f32[3,10,1,130]{3,2,1,0:T(1,128)S(1)}, u32[]{:S(2)}, u32[]{:S(2)}) collective-permute-start(f32[3,10,1,130]{3,2,1,0:T(1,128)S(1)} %get-tuple-element.21), channel_id=1, source_target_pairs={{0,1},{1,2},{2,3},{4,5},{5,6},{6,7},{8,9},{9,10},{10,11},{12,13},{... | collective-permute-start | bytes 46808 | tf_op jit(solution)/shard_map/ppermute | solution.py:20
where the time goes:
time: 190 us; the launch traced here: 188 us
  starting transfers between devices  82.7 us (44%)
  local copies, waits for them, and re-layouts  45.7 us (24%)
  waiting for transfers between devices  32.2 us (17%)
  other arithmetic  26 us (14%)
    ppermute x15, starting transfers between devices, padded_2(): lax.ppermute(lax.slice_in_dim(block, block.shape[dim] - width, None, axis...  55.1 us
    ppermute x15, starting transfers between devices, padded_2(): lax.ppermute(lax.slice_in_dim(block, 0, width, axis=dim), axis, backward)  23.3 us
    ppermute x15, waiting for transfers between devices, padded_2(): lax.ppermute(lax.slice_in_dim(block, 0, width, axis=dim), axis, backward)  23 us
    reshape x1, local copies, waits for them, and re-layouts, block_mean(): field.reshape(components, size_x // 2, 2, size_y // 2, 2, size_z // 2, 2)  14 us
    reshape x1, local copies, waits for them, and re-layouts, prolong(): return expanded.reshape(components, 2 * size_x, 2 * size_y, 2 * size_z)  9.76 us
    ppermute x15, waiting for transfers between devices, padded_2(): lax.ppermute(lax.slice_in_dim(block, block.shape[dim] - width, None, axis...  9.15 us
    reduce_sum x2, other arithmetic, block_mean(): field.reshape(components, size_x // 2, 2, size_y // 2, 2, size_z // 2, 2)  8.07 us
    another operation x1, local copies, waits for them, and re-layouts, block_mean(): field.reshape(components, size_x // 2, 2, size_y // 2, 2, size_z // 2, 2)  5.57 us
  transfers between devices with their start and end apart: 31, of which 13 were waited for; matrix products, arithmetic and copies ran while one was open for 27% of the time, Pallas kernels for 0%

commit v1 on v0

v1 whole, which is shorter than its diff:
```python
import functools

import jax
import jax.numpy as jnp
import numpy as np
from jax import lax
from jax.experimental import pallas as pl
from jax.experimental.pallas import tpu as pltpu
from jax.sharding import PartitionSpec as P

SWEEPS = 2
COARSE_SWEEPS = 4
LX = 5
MESH = pl.DeviceIdType.MESH

damping = 0.8
keep = 1.0 - damping
root_half = 0.7071067811865476


def local_levels(cells_x):
    return min(LX, cells_x.bit_length() - 1)


def finish_matrix(cells_x, blocks, rows):
    levels = local_levels(cells_x)
    kept = cells_x // 2
    eye = np.eye(blocks * kept).reshape(blocks, kept, blocks * kept)
    width = cells_x >> levels
    approx = eye[:, :width].reshape(blocks * width, -1)
    details, at = [], width
    for level in range(levels, 1, -1):
        width = cells_x >> level
        details.append(eye[:, at : at + width].reshape(blocks * width, -1))
        at += width
    for level in range(levels, LX):
        low, high = approx[0::2], approx[1::2]
        approx, detail = (low + high) * root_half, (low - high) * root_half
        details.insert(0, detail)
    along_x = np.concatenate([approx] + details, axis=0)
    along_y = np.zeros((rows, rows))
    for row in range(0, rows, 2):
        along_y[row, row : row + 2] = root_half
        along_y[row + 1, row : row + 2] = root_half, -root_half
    return np.einsum("qk,yr->kryq", along_x, along_y).reshape(blocks * kept * rows, -1).astype(np.float32)


def neighbour_sides():
    return [(axis, high) for axis in ("gx", "gy", "agg") for high in (False, True)]


def kernel(
    sizes, v_ref, f_ref, r_ref, m_ref, vel_ref, comp_ref,
    xs_fine, xr_fine, ys_fine, yr_fine, zs_fine, zr_fine,
    xs_coarse, xr_coarse, ys_coarse, yr_coarse, zs_coarse, zr_coarse,
    c_send, c_recv, w_buf, send_sem, recv_sem, c_send_sem, c_recv_sem,
):
    counts = sizes
    C, X, Y, Z = v_ref.shape
    Xc = X // 2
    half = Z // 2
    me = {axis: lax.axis_index(axis) for axis in counts}
    blocks = counts["gx"]
    chunk = Z // blocks

    def exists(axis, high):
        return me[axis] < counts[axis] - 1 if high else me[axis] > 0

    barrier = pltpu.get_barrier_semaphore()
    expected = blocks - 1
    for step in range(1, blocks):
        pl.semaphore_signal(
            barrier, inc=1, device_id={"gx": lax.rem(me["gx"] + step, blocks)}, device_id_type=MESH
        )
    for axis, high in neighbour_sides()[2:]:
        there = exists(axis, high)
        expected = expected + there.astype(jnp.int32)

        @pl.when(there)
        def _():
            pl.semaphore_signal(
                barrier, inc=1, device_id={axis: me[axis] + (1 if high else -1)}, device_id_type=MESH
            )

    received = {"gx": (xr_fine, xr_coarse), "gy": (yr_fine, yr_coarse), "agg": (zr_fine, zr_coarse)}
    for axis, high in neighbour_sides():
        @pl.when(jnp.logical_not(exists(axis, high)))
        def _():
            for buffer in received[axis]:
                for phase in range(buffer.shape[0]):
                    buffer[phase, int(high)] = jnp.zeros(buffer.shape[2:], buffer.dtype)

    row = lax.broadcasted_iota(jnp.int32, (Y, Z), 0)
    lane = lax.broadcasted_iota(jnp.int32, (Y, Z), 1)
    zero = jnp.zeros((Y, Z), jnp.float32)

    def pack(fields, width, phase, xs, ys, zs, store_x):
        if store_x:
            for c in range(C):
                xs[phase, 0, c] = fields[c][0]
                xs[phase, 1, c] = fields[c][width - 1]
        packed = zero
        for c in range(C):
            for x in range(width):
                k = c * width + x
                field = fields[c][x]
                ys[phase, 0, k : k + 1] = field[0:1]
                ys[phase, 1, k : k + 1] = field[Y - 1 : Y]
                packed = jnp.where(lane == k, field[:, 0:1], packed)
                packed = jnp.where(lane == half + k, field[:, Z - 1 : Z], packed)
        zs[phase] = packed

    def copies(fine, phase):
        number = phase if fine else SWEEPS + 1 + phase
        xs, xr, ys, yr, zs, zr = (
            (xs_fine, xr_fine, ys_fine, yr_fine, zs_fine, zr_fine)
            if fine
            else (xs_coarse, xr_coarse, ys_coarse, yr_coarse, zs_coarse, zr_coarse)
        )
        made = []
        for slot, (axis, high) in enumerate(neighbour_sides()):
            side = int(high)
            if axis == "gx":
                if fine and phase == 0:
                    src = v_ref.at[:, X - 1 if high else 0]
                else:
                    src = xs.at[phase, side]
                dst = xr.at[phase, 1 - side]
            elif axis == "gy":
                src, dst = ys.at[phase, side], yr.at[phase, 1 - side]
            else:
                src, dst = zs.at[phase], zr.at[phase, 1 - side]
            made.append((
                axis,
                high,
                pltpu.make_async_remote_copy(
                    src_ref=src,
                    dst_ref=dst,
                    send_sem=send_sem.at[number, slot],
                    recv_sem=recv_sem.at[number, slot],
                    device_id={axis: me[axis] + (1 if high else -1)},
                    device_id_type=MESH,
                ),
            ))
        return made

    def start(fine, phase):
        for axis, high, copy in copies(fine, phase):
            pl.when(exists(axis, high))(copy.start)

    def arrive(fine, phase):
        for axis, high, copy in copies(fine, phase):
            pl.when(exists(axis, not high))(copy.wait_recv)

    def sent(fine, phase):
        for axis, high, copy in copies(fine, phase):
            pl.when(exists(axis, high))(copy.wait_send)

    def inner_sum(fields, width, stride):
        sums = []
        for c in range(C):
            line = []
            for x in range(width):
                field = fields[c][x]
                total = jnp.where(row < stride, zero, pltpu.roll(field, stride, 0))
                total = total + jnp.where(row >= Y - stride, zero, pltpu.roll(field, Y - stride, 0))
                total = total + jnp.where(lane < stride, zero, pltpu.roll(field, stride, 1))
                total = total + jnp.where(lane >= Z - stride, zero, pltpu.roll(field, Z - stride, 1))
                if x > 0:
                    total = total + fields[c][x - 1]
                if x < width - 1:
                    total = total + fields[c][x + 1]
                line.append(total)
            sums.append(line)
        return sums

    def outer_sum(sums, width, stride, phase, xr, yr, zr, repeat=1):
        from_low, from_high = zr[phase, 0], zr[phase, 1]
        result = []
        for c in range(C):
            line = []
            for x in range(width):
                k = c * (width // repeat) + x // repeat
                total = sums[c][x]
                total = total + jnp.where(row < stride, yr[phase, 0, k : k + 1], 0.0)
                total = total + jnp.where(row >= Y - stride, yr[phase, 1, k : k + 1], 0.0)
                total = total + jnp.where(lane < stride, from_low[:, half + k : half + k + 1], 0.0)
                total = total + jnp.where(lane >= Z - stride, from_high[:, k : k + 1], 0.0)
                if x == 0:
                    total = total + xr[phase, 0, c]
                if x == width - 1:
                    total = total + xr[phase, 1, c]
                line.append(total)
            result.append(line)
        return result

    fine_recv = (xr_fine, yr_fine, zr_fine)
    coarse_recv = (xr_coarse, yr_coarse, zr_coarse)
    fine_send = (xs_fine, ys_fine, zs_fine)
    coarse_send = (xs_coarse, ys_coarse, zs_coarse)

    previous = [[v_ref[c, x] for x in range(X)] for c in range(C)]
    pack(previous, X, 0, *fine_send, False)
    pl.semaphore_wait(barrier, expected)
    start(True, 0)

    kept = X // 2
    levels = local_levels(X)
    even_row = row % 2 == 0
    even_lane = lane % 2 == 0
    combos_per_tile = Z // chunk
    coefficients = []
    for c in range(C):
        approx, details = previous[c], []
        for level in range(levels):
            low, high = approx[0::2], approx[1::2]
            approx = [(a + b) * root_half for a, b in zip(low, high)]
            if level > 0:
                details = [(a - b) * root_half for a, b in zip(low, high)] + details
        line = []
        for field in approx + details:
            swapped = jnp.where(even_lane, pltpu.roll(field, Z - 1, 1), pltpu.roll(field, 1, 1))
            line.append((jnp.where(even_lane, field, -field) + swapped) * root_half)
        coefficients.append(line)
    row8 = lax.broadcasted_iota(jnp.int32, (8, Z), 1)
    parts = Y // 8
    for j in range(blocks):
        for k in range(kept):
            tiles = {}
            for c in range(C):
                for part in range(parts):
                    tile, place = divmod(c * parts + part, combos_per_tile)
                    field = coefficients[c][k][part * 8 : part * 8 + 8]
                    shift = (place * chunk - j * chunk) % Z
                    moved = pltpu.roll(field, shift, 1) if shift else field
                    if tile in tiles:
                        moved = jnp.where((row8 >= place * chunk) & (row8 < (place + 1) * chunk), moved, tiles[tile])
                    tiles[tile] = moved
            for tile, value in tiles.items():
                c_send[j, tile, k] = value

    def c_copy(j, source):
        return pltpu.make_async_remote_copy(
            src_ref=c_send.at[j],
            dst_ref=c_recv.at[source],
            send_sem=c_send_sem.at[j],
            recv_sem=c_recv_sem.at[source],
            device_id={"gx": j},
            device_id_type=MESH,
        )

    for j in range(blocks):
        pl.when(me["gx"] != j)(c_copy(j, me["gx"]).start)

        @pl.when(me["gx"] == j)
        def _():
            c_recv[j] = c_send[j]

    def finish_compressed():
        for j in range(blocks):
            pl.when(me["gx"] != j)(c_copy(j, j).wait_recv)
        coefs = blocks * kept
        for tile in range(c_send.shape[1]):
            gathered = c_recv[:, tile].reshape(coefs * 8, Z)
            done = lax.dot_general(
                gathered, m_ref[...], (((0,), (0,)), ((), ())),
                precision=lax.Precision.HIGHEST, preferred_element_type=jnp.float32,
            )
            for place in range(combos_per_tile):
                c, part = divmod(tile * combos_per_tile + place, parts)
                if c < C:
                    for y in range(8):
                        comp_ref[c, part * 8 + y] = done[
                            place * chunk : (place + 1) * chunk, y * coefs : (y + 1) * coefs
                        ]

    diagonal = [6.0 + r_ref[x] for x in range(X)]
    for x in range(X):
        w_buf[x] = damping / diagonal[x]
    field = previous
    for sweep in range(SWEEPS):
        sums = inner_sum(field, X, 1)
        sums = [[sums[c][x] + f_ref[c, x] for x in range(X)] for c in range(C)]
        arrive(True, sweep)
        sums = outer_sum(sums, X, 1, sweep, *fine_recv)
        field = [[keep * field[c][x] + w_buf[x] * sums[c][x] for x in range(X)] for c in range(C)]
        pack(field, X, sweep + 1, *fine_send, True)
        start(True, sweep + 1)

    def pooled(planes):
        out = []
        for x in range(0, len(planes), 2):
            total = planes[x] + planes[x + 1]
            total = total + jnp.where(even_row, pltpu.roll(total, Y - 1, 0), pltpu.roll(total, 1, 0))
            total = total + jnp.where(even_lane, pltpu.roll(total, Z - 1, 1), pltpu.roll(total, 1, 1))
            out.append(total * 0.125)
        return out

    sums = inner_sum(field, X, 1)
    sums = [[sums[c][x] + f_ref[c, x] for x in range(X)] for c in range(C)]
    coarse_weight = [damping / ((6.0 + 4.0 * mean) * 0.25) for mean in pooled([r_ref[x] for x in range(X)])]
    arrive(True, SWEEPS)
    sums = outer_sum(sums, X, 1, SWEEPS, *fine_recv)
    coarse_rhs = [
        pooled([sums[c][x] - (6.0 + r_ref[x]) * field[c][x] for x in range(X)]) for c in range(C)
    ]
    correction = [[coarse_weight[x] * coarse_rhs[c][x] for x in range(Xc)] for c in range(C)]
    pack(correction, Xc, 0, *coarse_send, True)
    start(False, 0)
    finish_compressed()
    for step in range(COARSE_SWEEPS - 1):
        coarse_sums = inner_sum(correction, Xc, 2)
        arrive(False, step)
        coarse_sums = outer_sum(coarse_sums, Xc, 2, step, *coarse_recv)
        correction = [
            [
                keep * correction[c][x] + coarse_weight[x] * (coarse_rhs[c][x] + 0.25 * coarse_sums[c][x])
                for x in range(Xc)
            ]
            for c in range(C)
        ]
        pack(correction, Xc, step + 1, *coarse_send, True)
        start(False, step + 1)
    spread = [[correction[c][x // 2] for x in range(X)] for c in range(C)]
    added = inner_sum(spread, X, 1)
    sums = [[sums[c][x] + added[c][x] for x in range(X)] for c in range(C)]
    arrive(False, COARSE_SWEEPS - 1)
    sums = outer_sum(sums, X, 1, COARSE_SWEEPS - 1, *coarse_recv, repeat=2)
    for c in range(C):
        for x in range(X):
            vel_ref[c, x] = keep * (field[c][x] + spread[c][x]) + w_buf[x] * sums[c][x]

    for phase in range(SWEEPS + 1):
        sent(True, phase)
    for phase in range(COARSE_SWEEPS):
        sent(False, phase)
    for j in range(blocks):
        pl.when(me["gx"] != j)(c_copy(j, me["gx"]).wait_send)


def on_device(counts, velocity_prev, forcing, reaction):
    C, X, Y, Z = velocity_prev.shape
    blocks = counts["gx"]
    kept = X // 2
    chunk = Z // blocks
    tiles = -(-(C * (Y // 8)) // (Z // chunk))
    matrix = jnp.asarray(finish_matrix(X, blocks, 8))
    vmem = pl.BlockSpec(memory_space=pltpu.VMEM)

    def buffers(phases, width):
        return [
            pltpu.VMEM((phases, 2, C, Y, Z), jnp.float32),
            pltpu.VMEM((phases, 2, C, Y, Z), jnp.float32),
            pltpu.VMEM((phases, 2, C * width, Z), jnp.float32),
            pltpu.VMEM((phases, 2, C * width, Z), jnp.float32),
            pltpu.VMEM((phases, Y, Z), jnp.float32),
            pltpu.VMEM((phases, 2, Y, Z), jnp.float32),
        ]

    phases = SWEEPS + 1 + COARSE_SWEEPS
    return pl.pallas_call(
        functools.partial(kernel, counts),
        out_shape=(
            jax.ShapeDtypeStruct((C, X, Y, Z), jnp.float32),
            jax.ShapeDtypeStruct((C, Y, chunk, kept * blocks), jnp.float32),
        ),
        in_specs=[vmem] * 4,
        out_specs=(vmem, vmem),
        scratch_shapes=buffers(SWEEPS + 1, X) + buffers(COARSE_SWEEPS, X // 2) + [
            pltpu.VMEM((blocks, tiles, kept, 8, Z), jnp.float32),
            pltpu.VMEM((blocks, tiles, kept, 8, Z), jnp.float32),
            pltpu.VMEM((X, Y, Z), jnp.float32),
            pltpu.SemaphoreType.DMA((phases, 6)),
            pltpu.SemaphoreType.DMA((phases, 6)),
            pltpu.SemaphoreType.DMA((blocks,)),
            pltpu.SemaphoreType.DMA((blocks,)),
        ],
        compiler_params=pltpu.CompilerParams(collective_id=0, has_side_effects=True),
    )(velocity_prev, forcing, reaction, matrix)


def solution(mesh):
    counts = {axis: mesh.shape[axis] for axis in ("agg", "gx", "gy")}
    placed = (P(None, "gx", "gy", "agg"), P(None, "gx", "gy", "agg"), P("gx", "gy", "agg"))
    return jax.shard_map(
        functools.partial(on_device, counts),
        mesh=mesh,
        in_specs=placed,
        out_specs=(P(None, "gx", "gy", "agg"), P(None, "gy", ("agg", "gx"), None)),
        check_vma=False,
    )
```

time: 190 us -> 32 us (0.17)
  starting transfers between devices: 82.7 us -> 0 us
  local copies, waits for them, and re-layouts: 45.7 us -> 2.86 us
  waiting for transfers between devices: 32.2 us -> 0 us
  Pallas kernels: 0 us -> 28 us
  other arithmetic: 26 us -> 0 us
    ppermute x30 -> x0, starting transfers between devices: 78.4 us -> none  [the longest x15 55.1 us: padded_2(): lax.ppermute(lax.slice_in_dim(block, block.shape[dim] - width, None, axis...]
    ppermute x30 -> x0, waiting for transfers between devices: 32.2 us -> none  [the longest x15 23 us: padded_2(): lax.ppermute(lax.slice_in_dim(block, 0, width, axis=dim), axis, backward)]
    pallas_call x0 -> x1, Pallas kernels: none -> 28 us  [on_device(): pl.pallas_call(functools.partial(kernel, counts), out_shape=(jax.ShapeDty...]
    reshape x2 -> x0, local copies, waits for them, and re-layouts: 23.8 us -> none  [the longest x1 14 us: block_mean(): field.reshape(components, size_x // 2, 2, size_y // 2, 2, size_z // 2, 2)]
    reduce_sum x2 -> x0, other arithmetic: 8.07 us -> none  [block_mean(): field.reshape(components, size_x // 2, 2, size_y // 2, 2, size_z // 2, 2)]
    add x8 -> x0, other arithmetic: 6.55 us -> none  [the longest x2 3.06 us: on_device(): center + trim_cells(inside, shrink) * damping * residual_in / diagonal_in]
    another operation x1 -> x0, local copies, waits for them, and re-layouts: 5.57 us -> none  [block_mean(): field.reshape(components, size_x // 2, 2, size_y // 2, 2, size_z // 2, 2)]
    broadcast_in_dim x1 -> x0, local copies, waits for them, and re-layouts: 5.26 us -> none  [prolong(): jnp.broadcast_to(coarse[:, :, None, :, None, :, None], (components, size_...]
  transfers between devices with their start and end apart: 31 -> 0, of which waited for: 13 -> 0; matrix products, arithmetic and copies ran while one was open for 27% -> 0% of each run, Pallas kernels for 0% -> 0%
where the time goes in v1:
time: 32 us; the launch traced here: 31.5 us
  Pallas kernels  28 us (88%)
  local copies, waits for them, and re-layouts  2.86 us (9%)
  between operations  0.65 us (2%)
    pallas_call x1, Pallas kernels, on_device(): pl.pallas_call(functools.partial(kernel, counts), out_shape=(jax.ShapeDty...  28 us
    pallas_call x1, local copies, waits for them, and re-layouts, on_device(): pl.pallas_call(functools.partial(kernel, counts), out_shape=(jax.ShapeDty...  2.18 us
    unnamed x3, local copies, waits for them, and re-layouts  0.68 us

profile of v1, /device:TPU:1, one launch (start us, length us, event | category | flops | bytes accessed | tf_op | source)
XLA Modules:
  0.0 31.5 jit_solution(3443699689433521857)
XLA Ops:
  0.6 28.0 %shard_map.59 = (f32[3,8,16,128]{3,2,1,0:T(8,128)}, f32[3,16,32,16]{3,2,1,0:T(8,128)}) custom-call(f32[3,8,16,128]{3,2,1,0:T(8,128)} %v_ref.1, f32[3,8,16,128]{3,2,1,0:T(8,128)} %f_ref.1, f32[8,16,128]{2,1,0:T(8,128)} %r_ref.1, f32[128,128]{1,0:T(8,128)} %constant.2.clone.m_ref), custom_call_target="tpu_custom_call" | custom-call | tf_op jit(solution)/shard_map/pallas_call | solution.py:361
  28.6 0.0 copy-start
  28.6 2.2 %copy.6 = f32[3,16,32,16]{2,3,1,0:T(8,128)} copy(f32[3,16,32,16]{3,2,1,0:T(8,128)} %get-tuple-element.3) | data formatting | bytes 196608 | tf_op jit(solution)/shard_map/pallas_call | solution.py:361
  30.8 0.0 copy-done
  30.8 0.7 %copy.8 = f32[3,8,16,128]{3,2,1,0:T(8,128)} copy(f32[3,8,16,128]{3,2,1,0:T(8,128)S(1)} %copy-done) | data formatting | bytes 393216
Async XLA Ops:
  28.6 2.2 %copy-start = (f32[3,8,16,128]{3,2,1,0:T(8,128)S(1)}, f32[3,8,16,128]{3,2,1,0:T(8,128)}, u32[]{:S(2)}) copy-start(f32[3,8,16,128]{3,2,1,0:T(8,128)} %get-tuple-element.6) | copy-start | bytes 589828

commit v2 on v1

--- a/solution.py
+++ b/solution.py
@@ -42,7 +42,7 @@
     for row in range(0, rows, 2):
         along_y[row, row : row + 2] = root_half
         along_y[row + 1, row : row + 2] = root_half, -root_half
-    return np.einsum("qk,yr->kryq", along_x, along_y).reshape(blocks * kept * rows, -1).astype(np.float32)
+    return np.einsum("qk,yr->yqkr", along_x, along_y).reshape(-1, blocks * kept * rows).astype(np.float32)
 
 
 def neighbour_sides():
@@ -50,10 +50,10 @@
 
 
 def kernel(
-    sizes, v_ref, f_ref, r_ref, m_ref, vel_ref, comp_ref,
+    sizes, v_hbm, f_hbm, r_hbm, m_hbm, vel_ref, comp_ref, v_ref, f_ref, r_ref, m_ref,
     xs_fine, xr_fine, ys_fine, yr_fine, zs_fine, zr_fine,
     xs_coarse, xr_coarse, ys_coarse, yr_coarse, zs_coarse, zr_coarse,
-    c_send, c_recv, w_buf, send_sem, recv_sem, c_send_sem, c_recv_sem,
+    c_send, c_recv, w_buf, send_sem, recv_sem, c_send_sem, c_recv_sem, in_sem,
 ):
     counts = sizes
     C, X, Y, Z = v_ref.shape
@@ -66,6 +66,14 @@
     def exists(axis, high):
         return me[axis] < counts[axis] - 1 if high else me[axis] > 0
 
+    loads = [
+        pltpu.make_async_copy(src, dst, in_sem.at[i])
+        for i, (src, dst) in enumerate(
+            ((v_hbm, v_ref), (f_hbm, f_ref), (r_hbm, r_ref), (m_hbm, m_ref))
+        )
+    ]
+    for load in loads:
+        load.start()
     barrier = pltpu.get_barrier_semaphore()
     expected = blocks - 1
     for step in range(1, blocks):
@@ -94,11 +102,7 @@
     lane = lax.broadcasted_iota(jnp.int32, (Y, Z), 1)
     zero = jnp.zeros((Y, Z), jnp.float32)
 
-    def pack(fields, width, phase, xs, ys, zs, store_x):
-        if store_x:
-            for c in range(C):
-                xs[phase, 0, c] = fields[c][0]
-                xs[phase, 1, c] = fields[c][width - 1]
+    def pack(fields, width, phase, xs, ys, zs):
         packed = zero
         for c in range(C):
             for x in range(width):
@@ -144,9 +148,19 @@
             ))
         return made
 
-    def start(fine, phase):
+    def start(fine, phase, axes=("gx", "gy", "agg")):
         for axis, high, copy in copies(fine, phase):
-            pl.when(exists(axis, high))(copy.start)
+            if axis in axes:
+                pl.when(exists(axis, high))(copy.start)
+
+    def send(fine, phase, fields, width):
+        xs, ys, zs = fine_send if fine else coarse_send
+        for c in range(C):
+            xs[phase, 0, c] = fields[c][0]
+            xs[phase, 1, c] = fields[c][width - 1]
+        start(fine, phase, ("gx",))
+        pack(fields, width, phase, xs, ys, zs)
+        start(fine, phase, ("gy", "agg"))
 
     def arrive(fine, phase):
         for axis, high, copy in copies(fine, phase):
@@ -199,8 +213,9 @@
     fine_send = (xs_fine, ys_fine, zs_fine)
     coarse_send = (xs_coarse, ys_coarse, zs_coarse)
 
+    loads[0].wait()
     previous = [[v_ref[c, x] for x in range(X)] for c in range(C)]
-    pack(previous, X, 0, *fine_send, False)
+    pack(previous, X, 0, *fine_send)
     pl.semaphore_wait(barrier, expected)
     start(True, 0)
 
@@ -259,11 +274,12 @@
     def finish_compressed():
         for j in range(blocks):
             pl.when(me["gx"] != j)(c_copy(j, j).wait_recv)
+        loads[3].wait()
         coefs = blocks * kept
         for tile in range(c_send.shape[1]):
             gathered = c_recv[:, tile].reshape(coefs * 8, Z)
             done = lax.dot_general(
-                gathered, m_ref[...], (((0,), (0,)), ((), ())),
+                m_ref[...], gathered, (((1,), (0,)), ((), ())),
                 precision=lax.Precision.HIGHEST, preferred_element_type=jnp.float32,
             )
             for place in range(combos_per_tile):
@@ -271,9 +287,11 @@
                 if c < C:
                     for y in range(8):
                         comp_ref[c, part * 8 + y] = done[
-                            place * chunk : (place + 1) * chunk, y * coefs : (y + 1) * coefs
+                            y * coefs : (y + 1) * coefs, place * chunk : (place + 1) * chunk
                         ]
 
+    loads[1].wait()
+    loads[2].wait()
     diagonal = [6.0 + r_ref[x] for x in range(X)]
     for x in range(X):
         w_buf[x] = damping / diagonal[x]
@@ -284,8 +302,7 @@
         arrive(True, sweep)
         sums = outer_sum(sums, X, 1, sweep, *fine_recv)
         field = [[keep * field[c][x] + w_buf[x] * sums[c][x] for x in range(X)] for c in range(C)]
-        pack(field, X, sweep + 1, *fine_send, True)
-        start(True, sweep + 1)
+        send(True, sweep + 1, field, X)
 
     def pooled(planes):
         out = []
@@ -305,8 +322,7 @@
         pooled([sums[c][x] - (6.0 + r_ref[x]) * field[c][x] for x in range(X)]) for c in range(C)
     ]
     correction = [[coarse_weight[x] * coarse_rhs[c][x] for x in range(Xc)] for c in range(C)]
-    pack(correction, Xc, 0, *coarse_send, True)
-    start(False, 0)
+    send(False, 0, correction, Xc)
     finish_compressed()
     for step in range(COARSE_SWEEPS - 1):
         coarse_sums = inner_sum(correction, Xc, 2)
@@ -319,8 +335,7 @@
             ]
             for c in range(C)
         ]
-        pack(correction, Xc, step + 1, *coarse_send, True)
-        start(False, step + 1)
+        send(False, step + 1, correction, Xc)
     spread = [[correction[c][x // 2] for x in range(X)] for c in range(C)]
     added = inner_sum(spread, X, 1)
     sums = [[sums[c][x] + added[c][x] for x in range(X)] for c in range(C)]
@@ -358,15 +373,20 @@
         ]
 
     phases = SWEEPS + 1 + COARSE_SWEEPS
-    return pl.pallas_call(
+    velocity, compressed = pl.pallas_call(
         functools.partial(kernel, counts),
         out_shape=(
             jax.ShapeDtypeStruct((C, X, Y, Z), jnp.float32),
-            jax.ShapeDtypeStruct((C, Y, chunk, kept * blocks), jnp.float32),
+            jax.ShapeDtypeStruct((C, Y, kept * blocks, chunk), jnp.float32),
         ),
-        in_specs=[vmem] * 4,
+        in_specs=[pl.BlockSpec(memory_space=pltpu.HBM)] * 4,
         out_specs=(vmem, vmem),
-        scratch_shapes=buffers(SWEEPS + 1, X) + buffers(COARSE_SWEEPS, X // 2) + [
+        scratch_shapes=[
+            pltpu.VMEM((C, X, Y, Z), jnp.float32),
+            pltpu.VMEM((C, X, Y, Z), jnp.float32),
+            pltpu.VMEM((X, Y, Z), jnp.float32),
+            pltpu.VMEM(matrix.shape, jnp.float32),
+        ] + buffers(SWEEPS + 1, X) + buffers(COARSE_SWEEPS, X // 2) + [
             pltpu.VMEM((blocks, tiles, kept, 8, Z), jnp.float32),
             pltpu.VMEM((blocks, tiles, kept, 8, Z), jnp.float32),
             pltpu.VMEM((X, Y, Z), jnp.float32),
@@ -374,9 +394,11 @@
             pltpu.SemaphoreType.DMA((phases, 6)),
             pltpu.SemaphoreType.DMA((blocks,)),
             pltpu.SemaphoreType.DMA((blocks,)),
+            pltpu.SemaphoreType.DMA((4,)),
         ],
-        compiler_params=pltpu.CompilerParams(collective_id=0, has_side_effects=True),
+        compiler_params=pltpu.CompilerParams(collective_id=0, has_side_effects=True, vmem_limit_bytes=24 * 2**20),
     )(velocity_prev, forcing, reaction, matrix)
+    return velocity, jnp.swapaxes(compressed, 2, 3)
 
 
 def solution(mesh):

time: 32 us -> 32.8 us (1.025)
  local copies, waits for them, and re-layouts: 2.86 us -> 4.95 us
  Pallas kernels: 28 us -> 26.6 us
    unnamed x3 -> x10, local copies, waits for them, and re-layouts: 0.68 us -> 4.95 us
    pallas_call x1 -> x0, local copies, waits for them, and re-layouts: 2.18 us -> none  [on_device(): pl.pallas_call(functools.partial(kernel, counts), out_shape=(jax.ShapeDty...]
    pallas_call x1, Pallas kernels: 28 us -> 26.6 us  [on_device(): pl.pallas_call(functools.partial(kernel, counts), out_shape=(jax.ShapeDty...]
where the time goes in v2:
time: 32.8 us; the launch traced here: 32.2 us
  Pallas kernels  26.6 us (81%)
  local copies, waits for them, and re-layouts  4.95 us (15%)
  between operations  0.65 us (2%)
    pallas_call x1, Pallas kernels, on_device(): pl.pallas_call(functools.partial(kernel, counts), out_shape=(jax.ShapeDty...  26.6 us
    unnamed x10, local copies, waits for them, and re-layouts  4.95 us

profile of v2, /device:TPU:1, one launch (start us, length us, event | category | flops | bytes accessed | tf_op | source)
XLA Modules:
  0.0 32.2 jit_solution(1454036919540805312)
XLA Ops:
  0.6 0.0 copy-start
  0.6 0.9 %copy-done = f32[3,8,16,128]{3,2,1,0:T(8,128)S(1)} copy-done((f32[3,8,16,128]{3,2,1,0:T(8,128)S(1)}, f32[3,8,16,128]{3,2,1,0:T(8,128)}, u32[]{:S(2)}) %copy-start) | copy-done | bytes 196632
  1.6 0.0 copy-start.1
  1.6 0.9 %copy-done.1 = f32[3,8,16,128]{3,2,1,0:T(8,128)S(1)} copy-done((f32[3,8,16,128]{3,2,1,0:T(8,128)S(1)}, f32[3,8,16,128]{3,2,1,0:T(8,128)}, u32[]{:S(2)}) %copy-start.1) | copy-done | bytes 196632
  2.5 0.0 copy-start.2
  2.5 0.8 %copy-done.2 = f32[8,16,128]{2,1,0:T(8,128)S(1)} copy-done((f32[8,16,128]{2,1,0:T(8,128)S(1)}, f32[8,16,128]{2,1,0:T(8,128)}, u32[]{:S(2)}) %copy-start.2) | copy-done | bytes 65560
  3.3 0.0 copy-start.3
  3.3 0.8 %copy-done.3 = f32[128,128]{1,0:T(8,128)S(1)} copy-done((f32[128,128]{1,0:T(8,128)S(1)}, f32[128,128]{1,0:T(8,128)}, u32[]{:S(2)}) %copy-start.3) | copy-done | bytes 65560
  4.2 26.6 %shard_map.59 = (f32[3,8,16,128]{3,2,1,0:T(8,128)S(1)}, f32[3,16,16,32]{3,2,1,0:T(8,128)S(1)}) custom-call(f32[3,8,16,128]{3,2,1,0:T(8,128)S(1)} %copy-done, f32[3,8,16,128]{3,2,1,0:T(8,128)S(1)} %copy-done.1, f32[8,16,128]{2,1,0:T(8,128)S(1)} %copy-done.2, f32[128,128]{1,0:T(8,128)S(1)} %copy-done.3), custom_call_target="tpu_custom_call" | custom-call | tf_op jit(solution)/shard_map/pallas_call | solution.py:376
  30.7 0.7 %copy.8 = f32[3,8,16,128]{3,2,1,0:T(8,128)} copy(f32[3,8,16,128]{3,2,1,0:T(8,128)S(1)} %get-tuple-element.8) | data formatting | bytes 393216
  31.4 0.7 %copy.9 = f32[3,16,32,16]{2,3,1,0:T(8,128)} copy(f32[3,16,32,16]{2,3,1,0:T(8,128)S(1)} %bitcast.1) | data formatting | bytes 196608
Async XLA Ops:
  0.6 0.9 %copy-start = (f32[3,8,16,128]{3,2,1,0:T(8,128)S(1)}, f32[3,8,16,128]{3,2,1,0:T(8,128)}, u32[]{:S(2)}) copy-start(f32[3,8,16,128]{3,2,1,0:T(8,128)} %v_hbm.1) | copy-start | bytes 589828
  1.6 0.9 %copy-start.1 = (f32[3,8,16,128]{3,2,1,0:T(8,128)S(1)}, f32[3,8,16,128]{3,2,1,0:T(8,128)}, u32[]{:S(2)}) copy-start(f32[3,8,16,128]{3,2,1,0:T(8,128)} %f_hbm.1) | copy-start | bytes 589828
  2.5 0.8 %copy-start.2 = (f32[8,16,128]{2,1,0:T(8,128)S(1)}, f32[8,16,128]{2,1,0:T(8,128)}, u32[]{:S(2)}) copy-start(f32[8,16,128]{2,1,0:T(8,128)} %r_hbm.1) | copy-start | bytes 196612
  3.3 0.8 %copy-start.3 = (f32[128,128]{1,0:T(8,128)S(1)}, f32[128,128]{1,0:T(8,128)}, u32[]{:S(2)}) copy-start(f32[128,128]{1,0:T(8,128)} %constant.2.clone.m_hbm) | copy-start | bytes 196612

commit v3 on v2

--- a/solution.py
+++ b/solution.py
@@ -49,11 +49,17 @@
     return [(axis, high) for axis in ("gx", "gy", "agg") for high in (False, True)]
 
 
+def edge_sides():
+    pairs = (("gx", "gy"), ("gx", "agg"), ("gy", "agg"))
+    return [((a, p), (b, q)) for a, b in pairs for p in (False, True) for q in (False, True)]
+
+
 def kernel(
     sizes, v_hbm, f_hbm, r_hbm, m_hbm, vel_ref, comp_ref, v_ref, f_ref, r_ref, m_ref,
     xs_fine, xr_fine, ys_fine, yr_fine, zs_fine, zr_fine,
     xs_coarse, xr_coarse, ys_coarse, yr_coarse, zs_coarse, zr_coarse,
-    c_send, c_recv, w_buf, send_sem, recv_sem, c_send_sem, c_recv_sem, in_sem,
+    xs_deep, xr_deep, ys_deep, yr_deep, zs_deep, zr_deep, exy, exz, eyz,
+c_send, c_recv, w_buf, send_sem, recv_sem, deep_send_sem, deep_recv_sem, c_send_sem, c_recv_sem, in_sem,
 ):
     counts = sizes
     C, X, Y, Z = v_ref.shape
@@ -74,6 +80,9 @@
     ]
     for load in loads:
         load.start()
+    def beside(*sides):
+        return {axis: me[axis] + (1 if high else -1) for axis, high in sides}
+
     barrier = pltpu.get_barrier_semaphore()
     expected = blocks - 1
     for step in range(1, blocks):
@@ -90,7 +99,31 @@
                 barrier, inc=1, device_id={axis: me[axis] + (1 if high else -1)}, device_id_type=MESH
             )
 
-    received = {"gx": (xr_fine, xr_coarse), "gy": (yr_fine, yr_coarse), "agg": (zr_fine, zr_coarse)}
+    for (axis_a, high_a), (axis_b, high_b) in edge_sides():
+        there = exists(axis_a, high_a) & exists(axis_b, high_b)
+        expected = expected + there.astype(jnp.int32)
+
+        @pl.when(there)
+        def _():
+            pl.semaphore_signal(
+                barrier, inc=1, device_id=beside((axis_a, high_a), (axis_b, high_b)), device_id_type=MESH
+            )
+
+    received = {
+        "gx": (xr_fine, xr_coarse, xr_deep),
+        "gy": (yr_fine, yr_coarse, yr_deep),
+        "agg": (zr_fine, zr_coarse, zr_deep),
+    }
+    edges = {("gx", "gy"): exy, ("gx", "agg"): exz, ("gy", "agg"): eyz}
+    for (axis_a, high_a), (axis_b, high_b) in edge_sides():
+        @pl.when(jnp.logical_not(exists(axis_a, high_a) & exists(axis_b, high_b)))
+        def _():
+            buffer = edges[axis_a, axis_b]
+            for phase in range(buffer.shape[0]):
+                buffer[phase, 2 * int(high_a) + int(high_b)] = jnp.zeros(buffer.shape[2:], buffer.dtype)
+
+    for buffer in (ys_coarse, ys_deep):
+        buffer[...] = jnp.zeros(buffer.shape, buffer.dtype)
     for axis, high in neighbour_sides():
         @pl.when(jnp.logical_not(exists(axis, high)))
         def _():
@@ -188,25 +221,183 @@
             sums.append(line)
         return sums
 
-    def outer_sum(sums, width, stride, phase, xr, yr, zr, repeat=1):
-        from_low, from_high = zr[phase, 0], zr[phase, 1]
+    def outer_sum(sums, width, stride, faces, repeat=1):
+        along_x, along_y, along_z = faces
         result = []
         for c in range(C):
             line = []
             for x in range(width):
                 k = c * (width // repeat) + x // repeat
                 total = sums[c][x]
-                total = total + jnp.where(row < stride, yr[phase, 0, k : k + 1], 0.0)
-                total = total + jnp.where(row >= Y - stride, yr[phase, 1, k : k + 1], 0.0)
-                total = total + jnp.where(lane < stride, from_low[:, half + k : half + k + 1], 0.0)
-                total = total + jnp.where(lane >= Z - stride, from_high[:, k : k + 1], 0.0)
+                total = total + jnp.where(row < stride, along_y[0][k : k + 1], 0.0)
+                total = total + jnp.where(row >= Y - stride, along_y[1][k : k + 1], 0.0)
+                total = total + jnp.where(lane < stride, along_z[0][:, k : k + 1], 0.0)
+                total = total + jnp.where(lane >= Z - stride, along_z[1][:, k : k + 1], 0.0)
                 if x == 0:
-                    total = total + xr[phase, 0, c]
+                    total = total + along_x[0][c]
                 if x == width - 1:
-                    total = total + xr[phase, 1, c]
+                    total = total + along_x[1][c]
                 line.append(total)
             result.append(line)
         return result
+
+    def faces_of(xr, yr, zr, phase):
+        return (
+            [[xr[phase, side, c] for c in range(C)] for side in range(2)],
+            [yr[phase, side] for side in range(2)],
+            [pltpu.roll(zr[phase, 0], half, 1), zr[phase, 1]],
+        )
+
+    group = Z // 4
+    far = {0: 2, 1: 0}
+
+    def deep_copies(phase):
+        made = []
+        for slot, (first, second) in enumerate(edge_sides()):
+            number = 2 * int(first[1]) + int(second[1])
+            back = 3 - number
+            if second[0] == "gy":
+                src, dst = ys_deep.at[phase, int(second[1]), 0], exy.at[phase, back]
+            else:
+                src, dst = zs_deep.at[phase], (exz if first[0] == "gx" else eyz).at[phase, back]
+            made.append(((first, second), src, dst, 6 + slot))
+        for slot, (axis, high) in enumerate(neighbour_sides()):
+            side = int(high)
+            if axis == "gx":
+                src, dst = xs_deep.at[phase, side], xr_deep.at[phase, 1 - side]
+            elif axis == "gy":
+                src, dst = ys_deep.at[phase, side], yr_deep.at[phase, 1 - side]
+            else:
+                src, dst = zs_deep.at[phase], zr_deep.at[phase, 1 - side]
+            made.append((((axis, high),), src, dst, slot))
+        return [
+            (
+                sides,
+                pltpu.make_async_remote_copy(
+                    src_ref=src,
+                    dst_ref=dst,
+                    send_sem=deep_send_sem.at[phase, slot],
+                    recv_sem=deep_recv_sem.at[phase, slot],
+                    device_id=beside(*sides),
+                    device_id_type=MESH,
+                ),
+            )
+            for sides, src, dst, slot in made
+        ]
+
+    def all_exist(sides, flip):
+        there = None
+        for axis, high in sides:
+            one = exists(axis, high != flip)
+            there = one if there is None else there & one
+        return there
+
+    def deep_send(phase, fields, width, stride):
+        for c in range(C):
+            for depth in range(2):
+                xs_deep[phase, 0, depth, c] = fields[c][depth]
+                xs_deep[phase, 1, depth, c] = fields[c][width - 1 - depth]
+        ready = deep_copies(phase)
+        for sides, copy in ready:
+            if len(sides) == 1 and sides[0][0] == "gx":
+                pl.when(all_exist(sides, False))(copy.start)
+        packed = zero
+        for c in range(C):
+            for x in range(width):
+                k = c * width + x
+                field = fields[c][x]
+                for depth in range(2):
+                    at = depth * stride
+                    ys_deep[phase, 0, depth, k : k + 1] = field[at : at + 1]
+                    ys_deep[phase, 1, depth, k : k + 1] = field[Y - 1 - at : Y - at]
+                    packed = jnp.where(lane == depth * group + k, field[:, at : at + 1], packed)
+                    packed = jnp.where(
+                        lane == (2 + depth) * group + k, field[:, Z - 1 - at : Z - at], packed
+                    )
+        zs_deep[phase] = packed
+        for sides, copy in ready:
+            if not (len(sides) == 1 and sides[0][0] == "gx"):
+                pl.when(all_exist(sides, False))(copy.start)
+
+    def deep_arrive(phase):
+        for sides, copy in deep_copies(phase):
+            pl.when(all_exist(sides, True))(copy.wait_recv)
+
+    def deep_sent(phase):
+        for sides, copy in deep_copies(phase):
+            pl.when(all_exist(sides, False))(copy.wait_send)
+
+    def lanes_from(packed, number, shift=0):
+        turn = (shift - number * group) % Z
+        return pltpu.roll(packed, turn, 1) if turn else packed
+
+    def deep_faces(phase):
+        return (
+            [[xr_deep[phase, side, 0, c] for c in range(C)] for side in range(2)],
+            [yr_deep[phase, side, 0] for side in range(2)],
+            [lanes_from(zr_deep[phase, side], far[side]) for side in range(2)],
+        )
+
+    def advance_faces(phase, fields, width, stride, faces, added, weight):
+        along_x, along_y, along_z = [], [], []
+        rows = ys_deep.shape[3]
+        k_row = lax.broadcasted_iota(jnp.int32, (rows, Z), 0)
+        k_lane = lax.broadcasted_iota(jnp.int32, (rows, Z), 1)
+        for side in range(2):
+            near = width - 1 if side == 0 else 0
+            planes = []
+            for c in range(C):
+                plane = faces[0][side][c]
+                k = c * width + near
+                total = xr_deep[phase, side, 1, c] + fields[c][0 if side == 0 else width - 1]
+                total = total + jnp.where(
+                    row < stride, exy[phase, 2 * side, k : k + 1], pltpu.roll(plane, stride, 0)
+                )
+                total = total + jnp.where(
+                    row >= Y - stride, exy[phase, 2 * side + 1, k : k + 1], pltpu.roll(plane, Y - stride, 0)
+                )
+                low = exz[phase, 2 * side][:, far[0] * group + k : far[0] * group + k + 1]
+                high = exz[phase, 2 * side + 1][:, far[1] * group + k : far[1] * group + k + 1]
+                total = total + jnp.where(lane < stride, low, pltpu.roll(plane, stride, 1))
+                total = total + jnp.where(lane >= Z - stride, high, pltpu.roll(plane, Z - stride, 1))
+                planes.append(keep * plane + added[0][side][c] + weight[0][side][c] * total)
+            along_x.append(planes)
+
+            layer = faces[1][side]
+            total = yr_deep[phase, side, 1] + ys_deep[phase, side, 0]
+            spot = k_row % width
+            total = total + jnp.where(
+                spot == 0, pltpu.roll(exy[phase, side], rows - (width - 1), 0), pltpu.roll(layer, 1, 0)
+            )
+            total = total + jnp.where(
+                spot == width - 1, pltpu.roll(exy[phase, 2 + side], width - 1, 0), pltpu.roll(layer, rows - 1, 0)
+            )
+            at = Y - 1 if side == 0 else 0
+            ends = []
+            for z_side in range(2):
+                line = eyz[phase, 2 * side + z_side, at : at + 1]
+                chosen = jnp.where(k_lane == far[z_side] * group + k_row, line, 0.0)
+                ends.append(jnp.sum(chosen, axis=1, keepdims=True))
+            total = total + jnp.where(k_lane < stride, ends[0], pltpu.roll(layer, stride, 1))
+            total = total + jnp.where(k_lane >= Z - stride, ends[1], pltpu.roll(layer, Z - stride, 1))
+            along_y.append(keep * layer + added[1][side] + weight[1][side] * total)
+
+            layer = faces[2][side]
+            total = lanes_from(zr_deep[phase, side], far[side] + 1)
+            total = total + lanes_from(zs_deep[phase], 2 - far[side])
+            low = lanes_from(eyz[phase, side], far[side])[Y - 1 : Y]
+            high = lanes_from(eyz[phase, 2 + side], far[side])[0:1]
+            total = total + jnp.where(row < stride, low, pltpu.roll(layer, stride, 0))
+            total = total + jnp.where(row >= Y - stride, high, pltpu.roll(layer, Y - stride, 0))
+            spot = lane % width
+            total = total + jnp.where(
+                spot == 0, lanes_from(exz[phase, side], far[side], 1 - width), pltpu.roll(layer, 1, 1)
+            )
+            total = total + jnp.where(
+                spot == width - 1, lanes_from(exz[phase, 2 + side], far[side], width - 1), pltpu.roll(layer, Z - 1, 1)
+            )
+            along_z.append(keep * layer + added[2][side] + weight[2][side] * total)
+        return along_x, along_y, along_z
 
     fine_recv = (xr_fine, yr_fine, zr_fine)
     coarse_recv = (xr_coarse, yr_coarse, zr_coarse)
@@ -295,15 +486,6 @@
     diagonal = [6.0 + r_ref[x] for x in range(X)]
     for x in range(X):
         w_buf[x] = damping / diagonal[x]
-    field = previous
-    for sweep in range(SWEEPS):
-        sums = inner_sum(field, X, 1)
-        sums = [[sums[c][x] + f_ref[c, x] for x in range(X)] for c in range(C)]
-        arrive(True, sweep)
-        sums = outer_sum(sums, X, 1, sweep, *fine_recv)
-        field = [[keep * field[c][x] + w_buf[x] * sums[c][x] for x in range(X)] for c in range(C)]
-        send(True, sweep + 1, field, X)
-
     def pooled(planes):
         out = []
         for x in range(0, len(planes), 2):
@@ -313,42 +495,61 @@
             out.append(total * 0.125)
         return out
 
+    coarse_weight = [damping / ((6.0 + 4.0 * mean) * 0.25) for mean in pooled([r_ref[x] for x in range(X)])]
+    coarse_step = [0.25 * weight for weight in coarse_weight]
+    send(False, 0, [coarse_step] * C, Xc)
+    field = previous
+    for sweep in range(SWEEPS):
+        sums = inner_sum(field, X, 1)
+        sums = [[sums[c][x] + f_ref[c, x] for x in range(X)] for c in range(C)]
+        arrive(True, sweep)
+        sums = outer_sum(sums, X, 1, faces_of(*fine_recv, sweep))
+        field = [[keep * field[c][x] + w_buf[x] * sums[c][x] for x in range(X)] for c in range(C)]
+        send(True, sweep + 1, field, X)
+
     sums = inner_sum(field, X, 1)
     sums = [[sums[c][x] + f_ref[c, x] for x in range(X)] for c in range(C)]
-    coarse_weight = [damping / ((6.0 + 4.0 * mean) * 0.25) for mean in pooled([r_ref[x] for x in range(X)])]
     arrive(True, SWEEPS)
-    sums = outer_sum(sums, X, 1, SWEEPS, *fine_recv)
+    sums = outer_sum(sums, X, 1, faces_of(*fine_recv, SWEEPS))
     coarse_rhs = [
         pooled([sums[c][x] - (6.0 + r_ref[x]) * field[c][x] for x in range(X)]) for c in range(C)
     ]
     correction = [[coarse_weight[x] * coarse_rhs[c][x] for x in range(Xc)] for c in range(C)]
-    send(False, 0, correction, Xc)
+    deep_send(0, correction, Xc, 2)
     finish_compressed()
-    for step in range(COARSE_SWEEPS - 1):
-        coarse_sums = inner_sum(correction, Xc, 2)
-        arrive(False, step)
-        coarse_sums = outer_sum(coarse_sums, Xc, 2, step, *coarse_recv)
-        correction = [
-            [
-                keep * correction[c][x] + coarse_weight[x] * (coarse_rhs[c][x] + 0.25 * coarse_sums[c][x])
-                for x in range(Xc)
-            ]
+
+    def coarse_sweep(current, faces):
+        total = outer_sum(inner_sum(current, Xc, 2), Xc, 2, faces)
+        return [
+            [keep * current[c][x] + first[c][x] + coarse_step[x] * total[c][x] for x in range(Xc)]
             for c in range(C)
         ]
-        send(False, step + 1, correction, Xc)
+
+    first = correction
+    arrive(False, 0)
+    step_faces = faces_of(*coarse_recv, 0)
+    deep_arrive(0)
+    first_faces = deep_faces(0)
+    later_faces = advance_faces(0, correction, Xc, 2, first_faces, first_faces, step_faces)
+    correction = coarse_sweep(coarse_sweep(correction, first_faces), later_faces)
+    deep_send(1, correction, Xc, 2)
+    deep_arrive(1)
+    faces = deep_faces(1)
+    later_faces = advance_faces(1, correction, Xc, 2, faces, first_faces, step_faces)
+    correction = coarse_sweep(correction, faces)
     spread = [[correction[c][x // 2] for x in range(X)] for c in range(C)]
     added = inner_sum(spread, X, 1)
     sums = [[sums[c][x] + added[c][x] for x in range(X)] for c in range(C)]
-    arrive(False, COARSE_SWEEPS - 1)
-    sums = outer_sum(sums, X, 1, COARSE_SWEEPS - 1, *coarse_recv, repeat=2)
+    sums = outer_sum(sums, X, 1, later_faces, repeat=2)
     for c in range(C):
         for x in range(X):
             vel_ref[c, x] = keep * (field[c][x] + spread[c][x]) + w_buf[x] * sums[c][x]
 
     for phase in range(SWEEPS + 1):
         sent(True, phase)
-    for phase in range(COARSE_SWEEPS):
-        sent(False, phase)
+    sent(False, 0)
+    for phase in range(COARSE_SWEEPS // 2):
+        deep_sent(phase)
     for j in range(blocks):
         pl.when(me["gx"] != j)(c_copy(j, me["gx"]).wait_send)
 
@@ -366,13 +567,27 @@
         return [
             pltpu.VMEM((phases, 2, C, Y, Z), jnp.float32),
             pltpu.VMEM((phases, 2, C, Y, Z), jnp.float32),
-            pltpu.VMEM((phases, 2, C * width, Z), jnp.float32),
-            pltpu.VMEM((phases, 2, C * width, Z), jnp.float32),
+            pltpu.VMEM((phases, 2, -(-C * width // 8) * 8, Z), jnp.float32),
+            pltpu.VMEM((phases, 2, -(-C * width // 8) * 8, Z), jnp.float32),
             pltpu.VMEM((phases, Y, Z), jnp.float32),
             pltpu.VMEM((phases, 2, Y, Z), jnp.float32),
         ]
 
-    phases = SWEEPS + 1 + COARSE_SWEEPS
+    def deep_buffers(phases, width):
+        rows = -(-C * width // 8) * 8
+        return [
+            pltpu.VMEM((phases, 2, 2, C, Y, Z), jnp.float32),
+            pltpu.VMEM((phases, 2, 2, C, Y, Z), jnp.float32),
+            pltpu.VMEM((phases, 2, 2, rows, Z), jnp.float32),
+            pltpu.VMEM((phases, 2, 2, rows, Z), jnp.float32),
+            pltpu.VMEM((phases, Y, Z), jnp.float32),
+            pltpu.VMEM((phases, 2, Y, Z), jnp.float32),
+            pltpu.VMEM((phases, 4, rows, Z), jnp.float32),
+            pltpu.VMEM((phases, 4, Y, Z), jnp.float32),
+            pltpu.VMEM((phases, 4, Y, Z), jnp.float32),
+        ]
+
+    phases = SWEEPS + 2
     velocity, compressed = pl.pallas_call(
         functools.partial(kernel, counts),
         out_shape=(
@@ -386,17 +601,19 @@
             pltpu.VMEM((C, X, Y, Z), jnp.float32),
             pltpu.VMEM((X, Y, Z), jnp.float32),
             pltpu.VMEM(matrix.shape, jnp.float32),
-        ] + buffers(SWEEPS + 1, X) + buffers(COARSE_SWEEPS, X // 2) + [
+        ] + buffers(SWEEPS + 1, X) + buffers(1, X // 2) + deep_buffers(COARSE_SWEEPS // 2, X // 2) + [
             pltpu.VMEM((blocks, tiles, kept, 8, Z), jnp.float32),
             pltpu.VMEM((blocks, tiles, kept, 8, Z), jnp.float32),
             pltpu.VMEM((X, Y, Z), jnp.float32),
             pltpu.SemaphoreType.DMA((phases, 6)),
             pltpu.SemaphoreType.DMA((phases, 6)),
+            pltpu.SemaphoreType.DMA((COARSE_SWEEPS // 2, 18)),
+            pltpu.SemaphoreType.DMA((COARSE_SWEEPS // 2, 18)),
             pltpu.SemaphoreType.DMA((blocks,)),
             pltpu.SemaphoreType.DMA((blocks,)),
             pltpu.SemaphoreType.DMA((4,)),
         ],
-        compiler_params=pltpu.CompilerParams(collective_id=0, has_side_effects=True, vmem_limit_bytes=24 * 2**20),
+        compiler_params=pltpu.CompilerParams(collective_id=0, has_side_effects=True, vmem_limit_bytes=67043328),
     )(velocity_prev, forcing, reaction, matrix)
     return velocity, jnp.swapaxes(compressed, 2, 3)
 

time: 32.8 us -> 27.9 us (0.85); the launches traced: 32.2 us -> 27.8 us
  local copies, waits for them, and re-layouts: 4.95 us -> 2.42 us
  Pallas kernels: 26.6 us -> 24.7 us
    unnamed x10 -> x4, local copies, waits for them, and re-layouts: 4.95 us -> 2.42 us
    pallas_call x1, Pallas kernels: 26.6 us -> 24.7 us  [on_device(): pl.pallas_call(functools.partial(kernel, counts), out_shape=(jax.ShapeDty...]
where the time goes in v3:
time: 27.9 us; the launch traced here: 27.8 us
  Pallas kernels  24.7 us (89%)
  local copies, waits for them, and re-layouts  2.42 us (9%)
  between operations  0.65 us (2%)
    pallas_call x1, Pallas kernels, on_device(): pl.pallas_call(functools.partial(kernel, counts), out_shape=(jax.ShapeDty...  24.7 us
    unnamed x4, local copies, waits for them, and re-layouts  2.42 us

profile of v3, /device:TPU:1, one launch (start us, length us, event | category | flops | bytes accessed | tf_op | source)
XLA Modules:
  0.0 27.8 jit_solution(16330242190754335276)
XLA Ops:
  0.6 24.7 %shard_map.59 = (f32[3,8,16,128]{3,2,1,0:T(8,128)}, f32[3,16,16,32]{3,2,1,0:T(8,128)}) custom-call(f32[3,8,16,128]{3,2,1,0:T(8,128)} %v_hbm.1, f32[3,8,16,128]{3,2,1,0:T(8,128)} %f_hbm.1, f32[8,16,128]{2,1,0:T(8,128)} %r_hbm.1, f32[128,128]{1,0:T(8,128)} %constant.2.clone.m_hbm), custom_call_target="tpu_custom_call" | custom-call | tf_op jit(solution)/shard_map/pallas_call | solution.py:591
  25.4 0.0 copy-start
  25.4 1.7 %copy.8 = f32[3,8,16,128]{3,2,1,0:T(8,128)} copy(f32[3,8,16,128]{3,2,1,0:T(8,128)} %get-tuple-element.8) | data formatting | bytes 393216
  27.0 0.0 copy-done
  27.0 0.7 %copy.9 = f32[3,16,32,16]{2,3,1,0:T(8,128)} copy(f32[3,16,32,16]{2,3,1,0:T(8,128)S(1)} %bitcast.1) | data formatting | bytes 196608
Async XLA Ops:
  25.4 1.7 %copy-start = (f32[3,16,16,32]{3,2,1,0:T(8,128)S(1)}, f32[3,16,16,32]{3,2,1,0:T(8,128)}, u32[]{:S(2)}) copy-start(f32[3,16,16,32]{3,2,1,0:T(8,128)} %get-tuple-element.5) | copy-start | bytes 294916

commit v4 on v3

--- a/solution.py
+++ b/solution.py
@@ -613,8 +613,8 @@
             pltpu.SemaphoreType.DMA((blocks,)),
             pltpu.SemaphoreType.DMA((4,)),
         ],
-        compiler_params=pltpu.CompilerParams(collective_id=0, has_side_effects=True, vmem_limit_bytes=67043328),
-    )(velocity_prev, forcing, reaction, matrix)
+        compiler_params=pltpu.CompilerParams(collective_id=0, has_side_effects=True, vmem_limit_bytes=40000000),
+    )(*(pltpu.with_memory_space_constraint(a, pltpu.HBM) for a in (velocity_prev, forcing, reaction, matrix)))
     return velocity, jnp.swapaxes(compressed, 2, 3)
 
 

time: 27.9 us -> 26.1 us (0.935)
  local copies, waits for them, and re-layouts: 2.42 us -> 1.42 us
  Pallas kernels: 24.7 us -> 23.9 us
    unnamed x4 -> x2, local copies, waits for them, and re-layouts: 2.42 us -> 1.42 us
    pallas_call x1, Pallas kernels: 24.7 us -> 23.9 us  [on_device(): pl.pallas_call(functools.partial(kernel, counts), out_shape=(jax.ShapeDty...]
where the time goes in v4:
time: 26.1 us; the launch traced here: 26 us
  Pallas kernels  23.9 us (92%)
  local copies, waits for them, and re-layouts  1.42 us (5%)
  between operations  0.64 us (2%)
    pallas_call x1, Pallas kernels, on_device(): pl.pallas_call(functools.partial(kernel, counts), out_shape=(jax.ShapeDty...  23.9 us
    unnamed x2, local copies, waits for them, and re-layouts  1.42 us

profile of v4, /device:TPU:1, one launch (start us, length us, event | category | flops | bytes accessed | tf_op | source)
XLA Modules:
  0.0 26.0 jit_solution(6665659049862123166)
XLA Ops:
  0.6 23.9 %shard_map.59 = (f32[3,8,16,128]{3,2,1,0:T(8,128)S(1)}, f32[3,16,16,32]{3,2,1,0:T(8,128)S(1)}) custom-call(f32[3,8,16,128]{3,2,1,0:T(8,128)} %v_hbm.1, f32[3,8,16,128]{3,2,1,0:T(8,128)} %f_hbm.1, f32[8,16,128]{2,1,0:T(8,128)} %r_hbm.1, f32[128,128]{1,0:T(8,128)} %constant.2.clone.m_hbm), custom_call_target="tpu_custom_call" | custom-call | tf_op jit(solution)/shard_map/pallas_call | solution.py:591
  24.6 0.7 %copy.8 = f32[3,8,16,128]{3,2,1,0:T(8,128)} copy(f32[3,8,16,128]{3,2,1,0:T(8,128)S(1)} %get-tuple-element.8) | data formatting | bytes 393216
  25.2 0.7 %copy.9 = f32[3,16,32,16]{2,3,1,0:T(8,128)} copy(f32[3,16,32,16]{2,3,1,0:T(8,128)S(1)} %bitcast.1) | data formatting | bytes 196608

commit v5 on v4

--- a/solution.py
+++ b/solution.py
@@ -251,13 +251,17 @@
     group = Z // 4
     far = {0: 2, 1: 0}
 
+    def rows_of(width):
+        return -(-C * width // 8) * 8
+
     def deep_copies(phase):
         made = []
+        rows = pl.ds(0, rows_of(X if phase == 0 else Xc))
         for slot, (first, second) in enumerate(edge_sides()):
             number = 2 * int(first[1]) + int(second[1])
             back = 3 - number
             if second[0] == "gy":
-                src, dst = ys_deep.at[phase, int(second[1]), 0], exy.at[phase, back]
+                src, dst = ys_deep.at[phase, int(second[1]), 0, rows], exy.at[phase, back, rows]
             else:
                 src, dst = zs_deep.at[phase], (exz if first[0] == "gx" else eyz).at[phase, back]
             made.append(((first, second), src, dst, 6 + slot))
@@ -266,7 +270,7 @@
             if axis == "gx":
                 src, dst = xs_deep.at[phase, side], xr_deep.at[phase, 1 - side]
             elif axis == "gy":
-                src, dst = ys_deep.at[phase, side], yr_deep.at[phase, 1 - side]
+                src, dst = ys_deep.at[phase, side, :, rows], yr_deep.at[phase, 1 - side, :, rows]
             else:
                 src, dst = zs_deep.at[phase], zr_deep.at[phase, 1 - side]
             made.append((((axis, high),), src, dst, slot))
@@ -334,13 +338,13 @@
     def deep_faces(phase):
         return (
             [[xr_deep[phase, side, 0, c] for c in range(C)] for side in range(2)],
-            [yr_deep[phase, side, 0] for side in range(2)],
+            [yr_deep[phase, side, 0, : rows_of(X if phase == 0 else Xc)] for side in range(2)],
             [lanes_from(zr_deep[phase, side], far[side]) for side in range(2)],
         )
 
     def advance_faces(phase, fields, width, stride, faces, added, weight):
         along_x, along_y, along_z = [], [], []
-        rows = ys_deep.shape[3]
+        rows = rows_of(width)
         k_row = lax.broadcasted_iota(jnp.int32, (rows, Z), 0)
         k_lane = lax.broadcasted_iota(jnp.int32, (rows, Z), 1)
         for side in range(2):
@@ -364,13 +368,13 @@
             along_x.append(planes)
 
             layer = faces[1][side]
-            total = yr_deep[phase, side, 1] + ys_deep[phase, side, 0]
+            total = yr_deep[phase, side, 1, :rows] + ys_deep[phase, side, 0, :rows]
             spot = k_row % width
             total = total + jnp.where(
-                spot == 0, pltpu.roll(exy[phase, side], rows - (width - 1), 0), pltpu.roll(layer, 1, 0)
+                spot == 0, pltpu.roll(exy[phase, side, :rows], rows - (width - 1), 0), pltpu.roll(layer, 1, 0)
             )
             total = total + jnp.where(
-                spot == width - 1, pltpu.roll(exy[phase, 2 + side], width - 1, 0), pltpu.roll(layer, rows - 1, 0)
+                spot == width - 1, pltpu.roll(exy[phase, 2 + side, :rows], width - 1, 0), pltpu.roll(layer, rows - 1, 0)
             )
             at = Y - 1 if side == 0 else 0
             ends = []
@@ -409,6 +413,14 @@
     pack(previous, X, 0, *fine_send)
     pl.semaphore_wait(barrier, expected)
     start(True, 0)
+
+    loads[1].wait()
+    loads[2].wait()
+    for x in range(X):
+        w_buf[x] = damping / (6.0 + r_ref[x])
+    scaled = [[w_buf[x] * f_ref[c, x] for x in range(X)] for c in range(C)]
+    send(True, 1, scaled, X)
+    send(True, 2, [[w_buf[x] for x in range(X)]] * C, X)
 
     kept = X // 2
     levels = local_levels(X)
@@ -455,13 +467,6 @@
             device_id_type=MESH,
         )
 
-    for j in range(blocks):
-        pl.when(me["gx"] != j)(c_copy(j, me["gx"]).start)
-
-        @pl.when(me["gx"] == j)
-        def _():
-            c_recv[j] = c_send[j]
-
     def finish_compressed():
         for j in range(blocks):
             pl.when(me["gx"] != j)(c_copy(j, j).wait_recv)
@@ -481,11 +486,6 @@
                             y * coefs : (y + 1) * coefs, place * chunk : (place + 1) * chunk
                         ]
 
-    loads[1].wait()
-    loads[2].wait()
-    diagonal = [6.0 + r_ref[x] for x in range(X)]
-    for x in range(X):
-        w_buf[x] = damping / diagonal[x]
     def pooled(planes):
         out = []
         for x in range(0, len(planes), 2):
@@ -497,25 +497,41 @@
 
     coarse_weight = [damping / ((6.0 + 4.0 * mean) * 0.25) for mean in pooled([r_ref[x] for x in range(X)])]
     coarse_step = [0.25 * weight for weight in coarse_weight]
+
+    def fine_sums(current):
+        inner = inner_sum(current, X, 1)
+        return [[inner[c][x] + f_ref[c, x] for x in range(X)] for c in range(C)]
+
+    def fine_sweep(current, total):
+        return [[keep * current[c][x] + w_buf[x] * total[c][x] for x in range(X)] for c in range(C)]
+
+    sums = fine_sums(previous)
+    arrive(True, 0)
+    field = fine_sweep(previous, outer_sum(sums, X, 1, faces_of(*fine_recv, 0)))
+    deep_send(0, field, X, 1)
     send(False, 0, [coarse_step] * C, Xc)
-    field = previous
-    for sweep in range(SWEEPS):
-        sums = inner_sum(field, X, 1)
-        sums = [[sums[c][x] + f_ref[c, x] for x in range(X)] for c in range(C)]
-        arrive(True, sweep)
-        sums = outer_sum(sums, X, 1, faces_of(*fine_recv, sweep))
-        field = [[keep * field[c][x] + w_buf[x] * sums[c][x] for x in range(X)] for c in range(C)]
-        send(True, sweep + 1, field, X)
-
-    sums = inner_sum(field, X, 1)
-    sums = [[sums[c][x] + f_ref[c, x] for x in range(X)] for c in range(C)]
-    arrive(True, SWEEPS)
-    sums = outer_sum(sums, X, 1, faces_of(*fine_recv, SWEEPS))
+    for j in range(blocks):
+        pl.when(me["gx"] != j)(c_copy(j, me["gx"]).start)
+
+        @pl.when(me["gx"] == j)
+        def _():
+            c_recv[j] = c_send[j]
+
+    sums = fine_sums(field)
+    arrive(True, 1)
+    arrive(True, 2)
+    deep_arrive(0)
+    faces = deep_faces(0)
+    later_faces = advance_faces(
+        0, field, X, 1, faces, faces_of(*fine_recv, 1), faces_of(*fine_recv, 2)
+    )
+    field = fine_sweep(field, outer_sum(sums, X, 1, faces))
+    sums = outer_sum(fine_sums(field), X, 1, later_faces)
     coarse_rhs = [
         pooled([sums[c][x] - (6.0 + r_ref[x]) * field[c][x] for x in range(X)]) for c in range(C)
     ]
     correction = [[coarse_weight[x] * coarse_rhs[c][x] for x in range(Xc)] for c in range(C)]
-    deep_send(0, correction, Xc, 2)
+    deep_send(1, correction, Xc, 2)
     finish_compressed()
 
     def coarse_sweep(current, faces):
@@ -528,14 +544,14 @@
     first = correction
     arrive(False, 0)
     step_faces = faces_of(*coarse_recv, 0)
-    deep_arrive(0)
-    first_faces = deep_faces(0)
-    later_faces = advance_faces(0, correction, Xc, 2, first_faces, first_faces, step_faces)
+    deep_arrive(1)
+    first_faces = deep_faces(1)
+    later_faces = advance_faces(1, correction, Xc, 2, first_faces, first_faces, step_faces)
     correction = coarse_sweep(coarse_sweep(correction, first_faces), later_faces)
-    deep_send(1, correction, Xc, 2)
-    deep_arrive(1)
-    faces = deep_faces(1)
-    later_faces = advance_faces(1, correction, Xc, 2, faces, first_faces, step_faces)
+    deep_send(2, correction, Xc, 2)
+    deep_arrive(2)
+    faces = deep_faces(2)
+    later_faces = advance_faces(2, correction, Xc, 2, faces, first_faces, step_faces)
     correction = coarse_sweep(correction, faces)
     spread = [[correction[c][x // 2] for x in range(X)] for c in range(C)]
     added = inner_sum(spread, X, 1)
@@ -548,7 +564,7 @@
     for phase in range(SWEEPS + 1):
         sent(True, phase)
     sent(False, 0)
-    for phase in range(COARSE_SWEEPS // 2):
+    for phase in range(1 + COARSE_SWEEPS // 2):
         deep_sent(phase)
     for j in range(blocks):
         pl.when(me["gx"] != j)(c_copy(j, me["gx"]).wait_send)
@@ -601,14 +617,14 @@
             pltpu.VMEM((C, X, Y, Z), jnp.float32),
             pltpu.VMEM((X, Y, Z), jnp.float32),
             pltpu.VMEM(matrix.shape, jnp.float32),
-        ] + buffers(SWEEPS + 1, X) + buffers(1, X // 2) + deep_buffers(COARSE_SWEEPS // 2, X // 2) + [
+        ] + buffers(SWEEPS + 1, X) + buffers(1, X // 2) + deep_buffers(1 + COARSE_SWEEPS // 2, X) + [
             pltpu.VMEM((blocks, tiles, kept, 8, Z), jnp.float32),
             pltpu.VMEM((blocks, tiles, kept, 8, Z), jnp.float32),
             pltpu.VMEM((X, Y, Z), jnp.float32),
             pltpu.SemaphoreType.DMA((phases, 6)),
             pltpu.SemaphoreType.DMA((phases, 6)),
-            pltpu.SemaphoreType.DMA((COARSE_SWEEPS // 2, 18)),
-            pltpu.SemaphoreType.DMA((COARSE_SWEEPS // 2, 18)),
+            pltpu.SemaphoreType.DMA((1 + COARSE_SWEEPS // 2, 18)),
+            pltpu.SemaphoreType.DMA((1 + COARSE_SWEEPS // 2, 18)),
             pltpu.SemaphoreType.DMA((blocks,)),
             pltpu.SemaphoreType.DMA((blocks,)),
             pltpu.SemaphoreType.DMA((4,)),

time: 26.1 us -> 24.5 us (0.939)
  Pallas kernels: 23.9 us -> 22.1 us
    pallas_call x1, Pallas kernels: 23.9 us -> 22.1 us  [on_device(): pl.pallas_call(functools.partial(kernel, counts), out_shape=(jax.ShapeDty...]
where the time goes in v5:
time: 24.5 us; the launch traced here: 24.2 us
  Pallas kernels  22.1 us (90%)
  local copies, waits for them, and re-layouts  1.42 us (6%)
  between operations  0.64 us (3%)
    pallas_call x1, Pallas kernels, on_device(): pl.pallas_call(functools.partial(kernel, counts), out_shape=(jax.ShapeDty...  22.1 us
    unnamed x2, local copies, waits for them, and re-layouts  1.42 us

profile of v5, /device:TPU:1, one launch (start us, length us, event | category | flops | bytes accessed | tf_op | source)
XLA Modules:
  0.0 24.2 jit_solution(8660991707550090546)
XLA Ops:
  0.6 22.1 %shard_map.59 = (f32[3,8,16,128]{3,2,1,0:T(8,128)S(1)}, f32[3,16,16,32]{3,2,1,0:T(8,128)S(1)}) custom-call(f32[3,8,16,128]{3,2,1,0:T(8,128)} %v_hbm.1, f32[3,8,16,128]{3,2,1,0:T(8,128)} %f_hbm.1, f32[8,16,128]{2,1,0:T(8,128)} %r_hbm.1, f32[128,128]{1,0:T(8,128)} %constant.2.clone.m_hbm), custom_call_target="tpu_custom_call" | custom-call | tf_op jit(solution)/shard_map/pallas_call | solution.py:607
  22.8 0.7 %copy.8 = f32[3,8,16,128]{3,2,1,0:T(8,128)} copy(f32[3,8,16,128]{3,2,1,0:T(8,128)S(1)} %get-tuple-element.8) | data formatting | bytes 393216
  23.5 0.7 %copy.9 = f32[3,16,32,16]{2,3,1,0:T(8,128)} copy(f32[3,16,32,16]{2,3,1,0:T(8,128)S(1)} %bitcast.1) | data formatting | bytes 196608

commit v6 on v5

--- a/solution.py
+++ b/solution.py
@@ -423,10 +423,62 @@
     send(True, 2, [[w_buf[x] for x in range(X)]] * C, X)
 
     kept = X // 2
-    levels = local_levels(X)
+    parts = Y // 8
     even_row = row % 2 == 0
     even_lane = lane % 2 == 0
     combos_per_tile = Z // chunk
+    def c_copy(j, source):
+        return pltpu.make_async_remote_copy(
+            src_ref=c_send.at[j],
+            dst_ref=c_recv.at[source],
+            send_sem=c_send_sem.at[j],
+            recv_sem=c_recv_sem.at[source],
+            device_id={"gx": j},
+            device_id_type=MESH,
+        )
+
+    def finish_compressed(tiles):
+        coefs = blocks * kept
+        for tile in tiles:
+            gathered = c_recv[:, tile].reshape(coefs * 8, Z)
+            done = lax.dot_general(
+                m_ref[...], gathered, (((1,), (0,)), ((), ())),
+                precision=lax.Precision.HIGHEST, preferred_element_type=jnp.float32,
+            )
+            for place in range(combos_per_tile):
+                c, part = divmod(tile * combos_per_tile + place, parts)
+                if c < C:
+                    for y in range(8):
+                        comp_ref[c, part * 8 + y] = done[
+                            y * coefs : (y + 1) * coefs, place * chunk : (place + 1) * chunk
+                        ]
+
+    def pooled(planes):
+        out = []
+        for x in range(0, len(planes), 2):
+            total = planes[x] + planes[x + 1]
+            total = total + jnp.where(even_row, pltpu.roll(total, Y - 1, 0), pltpu.roll(total, 1, 0))
+            total = total + jnp.where(even_lane, pltpu.roll(total, Z - 1, 1), pltpu.roll(total, 1, 1))
+            out.append(total * 0.125)
+        return out
+
+    coarse_weight = [damping / ((6.0 + 4.0 * mean) * 0.25) for mean in pooled([r_ref[x] for x in range(X)])]
+    coarse_step = [0.25 * weight for weight in coarse_weight]
+
+    def fine_sums(current):
+        inner = inner_sum(current, X, 1)
+        return [[inner[c][x] + f_ref[c, x] for x in range(X)] for c in range(C)]
+
+    def fine_sweep(current, total):
+        return [[keep * current[c][x] + w_buf[x] * total[c][x] for x in range(X)] for c in range(C)]
+
+    sums = fine_sums(previous)
+    arrive(True, 0)
+    field = fine_sweep(previous, outer_sum(sums, X, 1, faces_of(*fine_recv, 0)))
+    deep_send(0, field, X, 1)
+    send(False, 0, [coarse_step] * C, Xc)
+
+    levels = local_levels(X)
     coefficients = []
     for c in range(C):
         approx, details = previous[c], []
@@ -436,80 +488,26 @@
             if level > 0:
                 details = [(a - b) * root_half for a, b in zip(low, high)] + details
         line = []
-        for field in approx + details:
-            swapped = jnp.where(even_lane, pltpu.roll(field, Z - 1, 1), pltpu.roll(field, 1, 1))
-            line.append((jnp.where(even_lane, field, -field) + swapped) * root_half)
+        for values in approx + details:
+            swapped = jnp.where(even_lane, pltpu.roll(values, Z - 1, 1), pltpu.roll(values, 1, 1))
+            line.append((jnp.where(even_lane, values, -values) + swapped) * root_half)
         coefficients.append(line)
     row8 = lax.broadcasted_iota(jnp.int32, (8, Z), 1)
-    parts = Y // 8
     for j in range(blocks):
         for k in range(kept):
             tiles = {}
             for c in range(C):
                 for part in range(parts):
                     tile, place = divmod(c * parts + part, combos_per_tile)
-                    field = coefficients[c][k][part * 8 : part * 8 + 8]
+                    values = coefficients[c][k][part * 8 : part * 8 + 8]
                     shift = (place * chunk - j * chunk) % Z
-                    moved = pltpu.roll(field, shift, 1) if shift else field
+                    moved = pltpu.roll(values, shift, 1) if shift else values
                     if tile in tiles:
                         moved = jnp.where((row8 >= place * chunk) & (row8 < (place + 1) * chunk), moved, tiles[tile])
                     tiles[tile] = moved
             for tile, value in tiles.items():
                 c_send[j, tile, k] = value
 
-    def c_copy(j, source):
-        return pltpu.make_async_remote_copy(
-            src_ref=c_send.at[j],
-            dst_ref=c_recv.at[source],
-            send_sem=c_send_sem.at[j],
-            recv_sem=c_recv_sem.at[source],
-            device_id={"gx": j},
-            device_id_type=MESH,
-        )
-
-    def finish_compressed():
-        for j in range(blocks):
-            pl.when(me["gx"] != j)(c_copy(j, j).wait_recv)
-        loads[3].wait()
-        coefs = blocks * kept
-        for tile in range(c_send.shape[1]):
-            gathered = c_recv[:, tile].reshape(coefs * 8, Z)
-            done = lax.dot_general(
-                m_ref[...], gathered, (((1,), (0,)), ((), ())),
-                precision=lax.Precision.HIGHEST, preferred_element_type=jnp.float32,
-            )
-            for place in range(combos_per_tile):
-                c, part = divmod(tile * combos_per_tile + place, parts)
-                if c < C:
-                    for y in range(8):
-                        comp_ref[c, part * 8 + y] = done[
-                            y * coefs : (y + 1) * coefs, place * chunk : (place + 1) * chunk
-                        ]
-
-    def pooled(planes):
-        out = []
-        for x in range(0, len(planes), 2):
-            total = planes[x] + planes[x + 1]
-            total = total + jnp.where(even_row, pltpu.roll(total, Y - 1, 0), pltpu.roll(total, 1, 0))
-            total = total + jnp.where(even_lane, pltpu.roll(total, Z - 1, 1), pltpu.roll(total, 1, 1))
-            out.append(total * 0.125)
-        return out
-
-    coarse_weight = [damping / ((6.0 + 4.0 * mean) * 0.25) for mean in pooled([r_ref[x] for x in range(X)])]
-    coarse_step = [0.25 * weight for weight in coarse_weight]
-
-    def fine_sums(current):
-        inner = inner_sum(current, X, 1)
-        return [[inner[c][x] + f_ref[c, x] for x in range(X)] for c in range(C)]
-
-    def fine_sweep(current, total):
-        return [[keep * current[c][x] + w_buf[x] * total[c][x] for x in range(X)] for c in range(C)]
-
-    sums = fine_sums(previous)
-    arrive(True, 0)
-    field = fine_sweep(previous, outer_sum(sums, X, 1, faces_of(*fine_recv, 0)))
-    deep_send(0, field, X, 1)
-    send(False, 0, [coarse_step] * C, Xc)
     for j in range(blocks):
         pl.when(me["gx"] != j)(c_copy(j, me["gx"]).start)
 
@@ -532,7 +530,12 @@
     ]
     correction = [[coarse_weight[x] * coarse_rhs[c][x] for x in range(Xc)] for c in range(C)]
     deep_send(1, correction, Xc, 2)
-    finish_compressed()
+    for j in range(blocks):
+        pl.when(me["gx"] != j)(c_copy(j, j).wait_recv)
+    loads[3].wait()
+    tiles_here = c_send.shape[1]
+    first_tiles = (tiles_here + 1) // 2
+    finish_compressed(range(first_tiles))
 
     def coarse_sweep(current, faces):
         total = outer_sum(inner_sum(current, Xc, 2), Xc, 2, faces)
@@ -549,6 +552,7 @@
     later_faces = advance_faces(1, correction, Xc, 2, first_faces, first_faces, step_faces)
     correction = coarse_sweep(coarse_sweep(correction, first_faces), later_faces)
     deep_send(2, correction, Xc, 2)
+    finish_compressed(range(first_tiles, tiles_here))
     deep_arrive(2)
     faces = deep_faces(2)
     later_faces = advance_faces(2, correction, Xc, 2, faces, first_faces, step_faces)

time: 24.5 us -> 24.5 us (level)
  no operation moved by 1% of the time
where the time goes in v6:
time: 24.5 us; the launch traced here: 24.2 us
  Pallas kernels  22.1 us (90%)
  local copies, waits for them, and re-layouts  1.42 us (6%)
  between operations  0.64 us (3%)
    pallas_call x1, Pallas kernels, on_device(): pl.pallas_call(functools.partial(kernel, counts), out_shape=(jax.ShapeDty...  22.1 us
    unnamed x2, local copies, waits for them, and re-layouts  1.42 us

profile of v6, /device:TPU:1, one launch (start us, length us, event | category | flops | bytes accessed | tf_op | source)
XLA Modules:
  0.0 24.2 jit_solution(8387570994135016464)
XLA Ops:
  0.6 22.1 %shard_map.59 = (f32[3,8,16,128]{3,2,1,0:T(8,128)S(1)}, f32[3,16,16,32]{3,2,1,0:T(8,128)S(1)}) custom-call(f32[3,8,16,128]{3,2,1,0:T(8,128)} %v_hbm.1, f32[3,8,16,128]{3,2,1,0:T(8,128)} %f_hbm.1, f32[8,16,128]{2,1,0:T(8,128)} %r_hbm.1, f32[128,128]{1,0:T(8,128)} %constant.2.clone.m_hbm), custom_call_target="tpu_custom_call" | custom-call | tf_op jit(solution)/shard_map/pallas_call | solution.py:611
  22.8 0.7 %copy.8 = f32[3,8,16,128]{3,2,1,0:T(8,128)} copy(f32[3,8,16,128]{3,2,1,0:T(8,128)S(1)} %get-tuple-element.8) | data formatting | bytes 393216
  23.5 0.7 %copy.9 = f32[3,16,32,16]{2,3,1,0:T(8,128)} copy(f32[3,16,32,16]{2,3,1,0:T(8,128)S(1)} %bitcast.1) | data formatting | bytes 196608

commit v7 on v6

--- a/solution.py
+++ b/solution.py
@@ -302,9 +302,6 @@
                 xs_deep[phase, 0, depth, c] = fields[c][depth]
                 xs_deep[phase, 1, depth, c] = fields[c][width - 1 - depth]
         ready = deep_copies(phase)
-        for sides, copy in ready:
-            if len(sides) == 1 and sides[0][0] == "gx":
-                pl.when(all_exist(sides, False))(copy.start)
         packed = zero
         for c in range(C):
             for x in range(width):
@@ -320,8 +317,7 @@
                     )
         zs_deep[phase] = packed
         for sides, copy in ready:
-            if not (len(sides) == 1 and sides[0][0] == "gx"):
-                pl.when(all_exist(sides, False))(copy.start)
+            pl.when(all_exist(sides, False))(copy.start)
 
     def deep_arrive(phase):
         for sides, copy in deep_copies(phase):

time: 24.5 us -> 24.3 us (level)
  no operation moved by 1% of the time
where the time goes in v7:
time: 24.3 us; the launch traced here: 24 us
  Pallas kernels  21.9 us (90%)
  local copies, waits for them, and re-layouts  1.42 us (6%)
  between operations  0.64 us (3%)
    pallas_call x1, Pallas kernels, on_device(): pl.pallas_call(functools.partial(kernel, counts), out_shape=(jax.ShapeDty...  21.9 us
    unnamed x2, local copies, waits for them, and re-layouts  1.42 us

profile of v7, /device:TPU:1, one launch (start us, length us, event | category | flops | bytes accessed | tf_op | source)
XLA Modules:
  0.0 24.0 jit_solution(7448711787001251484)
XLA Ops:
  0.6 21.9 %shard_map.59 = (f32[3,8,16,128]{3,2,1,0:T(8,128)S(1)}, f32[3,16,16,32]{3,2,1,0:T(8,128)S(1)}) custom-call(f32[3,8,16,128]{3,2,1,0:T(8,128)} %v_hbm.1, f32[3,8,16,128]{3,2,1,0:T(8,128)} %f_hbm.1, f32[8,16,128]{2,1,0:T(8,128)} %r_hbm.1, f32[128,128]{1,0:T(8,128)} %constant.2.clone.m_hbm), custom_call_target="tpu_custom_call" | custom-call | tf_op jit(solution)/shard_map/pallas_call | solution.py:607
  22.5 0.7 %copy.8 = f32[3,8,16,128]{3,2,1,0:T(8,128)} copy(f32[3,8,16,128]{3,2,1,0:T(8,128)S(1)} %get-tuple-element.8) | data formatting | bytes 393216
  23.2 0.7 %copy.9 = f32[3,16,32,16]{2,3,1,0:T(8,128)} copy(f32[3,16,32,16]{2,3,1,0:T(8,128)S(1)} %bitcast.1) | data formatting | bytes 196608
